TPU v7x, 256 devices: a 4x2x16 block of a 4x16x16 slice. The times are simulated.
256 devices in a mesh: grp: 2 (over y), gx: 16 (over z), gy: 4 (over x), gz: 2 (over core).
Axes of the slice: x: 4, y: 2, z: 16, core: 2. Of those that a mesh axis runs over, the one named last changes fastest.
The devices are a block of a 4x16x16 slice.
Arguments:
- observed: float32 [16384, 4, 256], P(('grp', 'gx', 'gy', 'gz')), parts along dimension 0, may hold values from -12 to 12
- predicted: float32 [16384, 4, 256], P(('grp', 'gx', 'gy', 'gz')), parts along dimension 0, may hold values from -6 to 6
- coherence_mask: int32 [16384, 256], P(('grp', 'gx', 'gy', 'gz')), parts along dimension 0, may hold values 0 or 1
- block_count: int32 [16384], P(('grp', 'gx', 'gy', 'gz')), parts along dimension 0, may hold values from 64 to 256
- block_owner: int32 [16384, 1], P(('grp', 'gx', 'gy', 'gz')), parts along dimension 0, may hold values from 0 to 63; in each aligned block of 64 rows (0 to 63, 64 to 127, ...) at most 4 rows name the same one
- block_matrix_choice: int32 [16384], P(('grp', 'gx', 'gy', 'gz')), parts along dimension 0, may hold values from 0 to 31
- block_patch: int32 [16384], P(('grp', 'gx', 'gy', 'gz')), parts along dimension 0, may hold values from 0 to 31
- look_vector: float32 [4, 3], replicated, may hold values from -1 to 1
- interp_weights: bfloat16 [32, 256, 128], replicated, may hold values from -0.375 to 0.375
- depth_kernel: float32 [64], P(('grp', 'gz')), parts along dimension 0, may hold values from 0.2 to 1
- stiffness: float32 [64, 512, 512], P(('grp', 'gz'), 'gx', 'gy'), parts along dimension 0, may hold values from 0.25 to 4
Outputs:
- adjoint_field: float32 [3, 64, 512, 512], P(None, ('grp', 'gz'), 'gx', 'gy'), parts along dimension 1
- cg_residual: float32 [3, 64, 512, 512], P(None, ('grp', 'gz'), 'gx', 'gy'), parts along dimension 1
There are 2 independent parts, one for each index of `grp`. A program takes and returns all parts, laid end to end along the dimension named above; an argument that names none is the same for every part. Nothing has to cross between parts.
Inputs may be any that keep to these rules, and one draw needn't show every extreme that they name: `block_owner`: the blocks of one device name no column tile more than 4 times; in some devices one tile is named exactly 4 times.
All inputs are finite; a program needn't handle non-finite values. No bound on the sum of `coherence_mask` on one device may be relied on, other than what follows from the above.
Results may differ from a plain program's by a relative error of at most 0.0029.
Values sent between devices are 32-bit elements; how exact they have to be, the bound alone decides.
A program may use at most 64 MiB of HBM per device.

v0:
```python
import jax
import jax.numpy as jnp
from jax import lax
from jax.experimental import pallas as pl
from jax.experimental.pallas import tpu as pltpu
from jax.sharding import PartitionSpec as P

EPOCHS = 4
PATCH_X = 8
PATCH_Y = 16
CAP = 4
EPS = 1e-06

SHIFT = 8.0
PRE = 1024.0
MOMENTS = 6

HIGHEST = lax.Precision.HIGHEST
F32 = jnp.float32


def roll(values, shift, axis):
    return pltpu.roll(values, shift % values.shape[axis], axis)


def ahead(values, axis):
    return roll(values, -1, axis)


def behind(values, axis):
    return roll(values, 1, axis)


def iota(shape, axis):
    return lax.broadcasted_iota(jnp.int32, shape, axis)


def product(first, second, moments):
    total = None
    for i, f in enumerate(first):
        for j, g in enumerate(second):
            term = f * g * moments[i + j]
            total = term if total is None else total + term
    return total


def combined(first, factor, second):
    size = max(len(first), len(second))
    out = []
    for i in range(size):
        value = first[i] if i < len(first) else None
        if i < len(second):
            term = factor * second[i]
            value = term if value is None else value + term
        out.append(value)
    return out


def applied(poly):
    out = []
    for i in range(len(poly) + 1):
        value = None
        for j in (i, i - 1):
            if 0 <= j < len(poly):
                value = poly[j] if value is None else value + poly[j]
        out.append(SHIFT * value)
    return out


def conjugate(moments):
    one = jnp.ones_like(moments[0])
    residual, direction, iterate = [one], [one], []
    now = moments[0]
    for step in range(3):
        image = applied(direction)
        alpha = now / product(direction, image, moments)
        scaled = [alpha * d for d in direction]
        iterate = scaled if not iterate else combined(iterate, one, scaled)
        residual = combined(residual, -alpha, image)
        if step < 2:
            new = product(residual, residual, moments)
            direction = combined(residual, new / now, direction)
            now = new
    return iterate, residual


def kernel(
    slots_ref, choice_ref, part_ref, depth_ref, stiff_ref,
    adj_ref, res_ref,
    got_slots, got_choice, flat_slots, flat_choice,
    surf, surf_other, halo_x, halo_y,
    stiff_x, wide_stiff, strip_out, strip_in, coef,
    depths, table,
    fields, w1, w2, div,
    row_out, row_in, ring_in,
    send_a2a, recv_a2a, send_sem, recv_sem,
):
    gx, gy, gz = lax.axis_index("gx"), lax.axis_index("gy"), lax.axis_index("gz")
    ngx, ngy = lax.axis_size("gx"), lax.axis_size("gy")
    owners = ngx * ngy
    me = gx * ngy + gy
    nz, nx, ny = stiff_ref.shape
    other = 1 - gz
    rows, lanes = nx + 8, 2 * ny
    tall = nx + 16

    def at(x, y, z):
        return {"gx": x, "gy": y, "gz": z}

    def wrap(value, count):
        return lax.rem(value + count, count)

    depths[...] = jnp.zeros(depths.shape, F32)
    depths[pl.ds(pl.multiple_of(8 + nz * gz, 8), nz), :] = depth_ref[...]

    barrier = pltpu.get_barrier_semaphore()

    def greet(k, carry):
        o = lax.rem(me + k, owners)
        pl.semaphore_signal(barrier, inc=1, device_id=at(o // ngy, lax.rem(o, ngy), gz))
        return carry

    lax.fori_loop(1, owners, greet, 0)
    for k in range(ngy):
        pl.semaphore_signal(barrier, inc=1, device_id=at(gx, wrap(gy + k, ngy), other))

    def domain(count):
        r, c = iota((count, lanes), 0), iota((count, lanes), 1)
        half = (count - nx) // 2
        in_x = (r < nx) | ((r < nx + half) & (gx < ngx - 1)) | ((r >= nx + half) & (gx > 0))
        in_y = (c < ny) | ((c < ny + ny // 2) & (gy < ngy - 1)) | ((c >= ny + ny // 2) & (gy > 0))
        return (in_x & in_y).astype(F32)

    zero_plane = jnp.zeros((rows, lanes), F32)
    for edge in (0, 2 * nz + 1):
        div[edge] = zero_plane
        for c in range(3):
            w1[c, edge] = zero_plane
            w2[c, edge] = zero_plane
    pl.semaphore_wait(barrier, owners - 1 + ngy)

    def remote(source, target, index, device):
        return pltpu.make_async_remote_copy(
            src_ref=source, dst_ref=target, send_sem=send_sem.at[index], recv_sem=recv_sem.at[index],
            device_id=device, device_id_type=pl.DeviceIdType.MESH,
        )

    x_up, x_down = wrap(gx + 1, ngx), wrap(gx - 1, ngx)
    y_up, y_down = wrap(gy + 1, ngy), wrap(gy - 1, ngy)
    own_depth = depth_ref
    early = [
        remote(stiff_ref.at[:, pl.ds(0, 8), :], stiff_x.at[0], 0, at(x_down, gy, gz)),
        remote(stiff_ref.at[:, pl.ds(nx - 8, 8), :], stiff_x.at[1], 1, at(x_up, gy, gz)),
        remote(own_depth, depths.at[pl.ds(pl.multiple_of(8 + nz * gz, 8), nz), :], 2, at(gx, gy, other)),
    ]
    for copy in early:
        copy.start()

    def post(k, carry):
        o = lax.rem(me + k, owners)
        device = at(o // ngy, lax.rem(o, ngy), gz)
        pltpu.make_async_remote_copy(
            src_ref=slots_ref.at[o], dst_ref=got_slots.at[me], send_sem=send_a2a.at[0], recv_sem=recv_a2a.at[0],
            device_id=device, device_id_type=pl.DeviceIdType.MESH,
        ).start()
        pltpu.make_async_remote_copy(
            src_ref=choice_ref.at[o], dst_ref=got_choice.at[me], send_sem=send_a2a.at[1], recv_sem=recv_a2a.at[1],
            device_id=device, device_id_type=pl.DeviceIdType.MESH,
        ).start()
        return carry

    lax.fori_loop(1, owners, post, 0)
    got_slots[me] = slots_ref[me]
    got_choice[me] = choice_ref[me]

    for copy in early:
        copy.wait()
    low = iota((8, ny), 0) < 4
    for z in range(nz):
        wide_stiff[z, 0:nx, :] = stiff_ref[z]
        wide_stiff[z, nx:rows, :] = jnp.where(low, stiff_x[0, z], stiff_x[1, z])
    turned = wide_stiff[...].reshape(nz * rows, ny).T
    strip_out[0] = turned[0:8]
    strip_out[1] = turned[ny - 8:ny]
    strips = [
        remote(strip_out.at[0], strip_in.at[0], 3, at(gx, y_down, gz)),
        remote(strip_out.at[1], strip_in.at[1], 4, at(gx, y_up, gz)),
    ]
    for copy in strips:
        copy.start()

    d = depths[...]
    where_z = iota(d.shape, 0)
    inside = ((where_z >= 8) & (where_z < 8 + 2 * nz)).astype(F32)
    d_up, d_down = ahead(d, 0), behind(d, 0)
    q = 0.5 * (d_up - d_down)
    kept_d, kept_q = inside * d, inside * q
    columns = (
        d,
        0.125 * (d_up + d_down),
        q,
        (1.0 / 32.0) * (ahead(kept_d, 0) - behind(kept_d, 0)),
        (1.0 / 32.0) * (ahead(kept_q, 0) - behind(kept_q, 0)),
    )
    for k, values in enumerate(columns):
        for z in range(2 * nz):
            table[k, z] = values[z + 8:z + 9]

    for copy in strips:
        copy.wait()
    filler = jnp.zeros((ny - 16, nz * rows), F32)
    beside = jnp.concatenate([strip_in[0], filler, strip_in[1]], axis=0).T.reshape(nz, rows, ny)
    base = nz * gz
    for z in range(nz):
        coef[base + z, :, 0:ny] = 0.125 * wide_stiff[z] - 0.25
        coef[base + z, :, ny:lanes] = 0.125 * beside[z] - 0.25
    passed = pl.ds((nz - 4) + 4 * gz, 4)
    layers = remote(coef.at[passed], coef.at[passed], 5, at(gx, gy, other))
    layers.start()

    for message, buffer in enumerate((slots_ref, choice_ref)):
        part = buffer.at[pl.ds(0, owners - 1)]
        pltpu.make_async_copy(part, part, send_a2a.at[message]).wait()
    for message, buffer in enumerate((got_slots, got_choice)):
        part = buffer.at[pl.ds(0, owners - 1)]
        pltpu.make_async_copy(part, part, recv_a2a.at[message]).wait()
    own_slot = iota((CAP, ny), 1) // (ny // CAP) == iota((CAP, ny), 0)
    for o in range(owners):
        for c in range(3):
            flat_slots[c, CAP * o:CAP * (o + 1), :] = got_slots[o, c]
        flat_choice[CAP * o:CAP * (o + 1), :] = jnp.where(own_slot, got_choice[o], 0.0)
    picked = flat_choice[...]
    tiles = []
    for c in range(3):
        spread = lax.dot_general(
            picked, flat_slots[c], (((0,), (0,)), ((), ())), precision=HIGHEST, preferred_element_type=F32
        )
        depth_places = ny // CAP
        placed = spread[0:depth_places]
        for j in range(1, CAP):
            placed = placed + spread[j * depth_places:(j + 1) * depth_places]
        tiles.append(placed)
    tile = jnp.concatenate(tiles, axis=0)
    sub = lax.rem(iota(tile.shape, 0), 8)
    chunk = iota(tile.shape, 1) // PATCH_Y
    for bit in (1, 2, 4):
        row_set, chunk_set = (sub // bit) % 2 == 1, (chunk // bit) % 2 == 1
        from_below = roll(roll(tile, -bit, 0), bit * PATCH_Y, 1)
        from_above = roll(roll(tile, bit, 0), -bit * PATCH_Y, 1)
        tile = jnp.where(row_set == chunk_set, tile, jnp.where(row_set, from_above, from_below))
    surf[0] = tile.reshape(3, nx, ny)
    swap = remote(surf.at[0], surf_other, 6, at(gx, gy, other))
    swap.start()
    swap.wait()
    surf[1] = surf[0] + surf_other[...]

    first, last = pl.ds(0, 8), pl.ds(nx - 8, 8)
    whole = surf.at[1]
    halos = [
        remote(whole.at[:, first, :], halo_x.at[0], 7, at(x_down, gy, gz)),
        remote(whole.at[:, last, :], halo_x.at[1], 8, at(x_up, gy, gz)),
        remote(whole.at[:, first, :], halo_x.at[2], 9, at(x_down, y_down, gz)),
        remote(whole.at[:, first, :], halo_x.at[3], 10, at(x_down, y_up, gz)),
        remote(whole.at[:, last, :], halo_x.at[4], 11, at(x_up, y_down, gz)),
        remote(whole.at[:, last, :], halo_x.at[5], 12, at(x_up, y_up, gz)),
        remote(whole, halo_y.at[0], 13, at(gx, y_down, gz)),
        remote(whole, halo_y.at[1], 14, at(gx, y_up, gz)),
    ]
    for copy in halos:
        copy.start()
    for copy in halos:
        copy.wait()
    mask_tall = domain(tall)
    mask = domain(rows)
    left = iota((1, ny), 1) < ny // 2
    low_rows = iota((8, lanes), 0) < 4

    def packed(values):
        return jnp.concatenate(
            [values[0:nx], jnp.where(low_rows, values[nx:nx + 8], values[nx + 8:nx + 16])], axis=0
        )

    around = []
    for c in range(3):
        main = jnp.concatenate([surf[1, c], halo_x[0, c], halo_x[1, c]], axis=0)
        side = jnp.concatenate(
            [
                jnp.where(left, halo_y[0, c], halo_y[1, c]),
                jnp.where(left, halo_x[2, c], halo_x[3, c]),
                jnp.where(left, halo_x[4, c], halo_x[5, c]),
            ],
            axis=0,
        )
        around.append(mask_tall * jnp.concatenate([main, side], axis=1))
    flux = mask_tall * (
        0.5 * ((ahead(around[0], 0) - behind(around[0], 0)) + (ahead(around[1], 1) - behind(around[1], 1)))
    )
    for c in range(3):
        s = around[c]
        beside_xy = (ahead(s, 0) + behind(s, 0)) + (ahead(s, 1) + behind(s, 1))
        fields[c] = packed(s)
        if c < 2:
            drop = 0.125 * beside_xy + (1.0 / 32.0) * (ahead(flux, c) - behind(flux, c))
            fields[3 + c] = mask * packed(drop)
            fields[6 + c] = mask * packed((1.0 / 32.0) * (ahead(around[2], c) - behind(around[2], c)))
        else:
            fields[3 + c] = mask * packed(0.125 * beside_xy)
    fields[8] = packed(flux)

    layers.wait()

    def first_layer(i, carry):
        z = (nz - 4) * gz + i
        value = [table[k, z] for k in range(5)]
        own = coef[z] * value[0] - value[1]
        for c in range(2):
            w1[c, z + 1] = mask * (fields[c] * own) - value[0] * fields[3 + c] - value[2] * fields[6 + c]
        w1[2, z + 1] = mask * (fields[2] * (own - value[4])) - value[0] * fields[5] - value[3] * fields[8]
        return carry

    lax.fori_loop(0, nz + 4, first_layer, 0)

    def spread_of(source, start, amount):
        def layer(i, carry):
            z = start + i
            x, y = source[0, z + 1], source[1, z + 1]
            div[z + 1] = mask * (
                ((ahead(x, 0) - behind(x, 0)) + (ahead(y, 1) - behind(y, 1)))
                + (source[2, z + 2] - source[2, z])
            )
            return carry

        lax.fori_loop(0, amount, layer, 0)

    spread_of(w1, (nz - 3) * gz, nz + 3)

    def second_layer(i, carry):
        z = (nz - 2) * gz + i
        own = coef[z]
        here = div[z + 1]
        for c in range(3):
            v = w1[c, z + 1]
            total = (ahead(v, 0) + behind(v, 0)) + (ahead(v, 1) + behind(v, 1))
            total = total + (w1[c, z + 2] + w1[c, z])
            slope = (ahead(here, c) - behind(here, c)) if c < 2 else (div[z + 2] - div[z])
            w2[c, z + 1] = mask * (own * v - 0.125 * total - (1.0 / 64.0) * slope)
        return carry

    lax.fori_loop(0, nz + 2, second_layer, 0)

    spread_of(w2, (nz - 1) * gz, nz + 1)

    def folded(values):
        total = values[0:8]
        for k in range(8, nx, 8):
            total = total + values[k:k + 8]
        return total

    def third_layer(i, sums):
        z = nz * gz + i
        own = coef[z, 0:nx, 0:ny]
        here_x, here_y = div[z + 1, :, 0:ny], div[z + 1, 0:nx, :]
        d_now = table[0, z, :, 0:ny]
        sums = list(sums)
        for c in range(3):
            v = w2[c, z + 1, 0:nx, 0:ny]
            vx, vy = w2[c, z + 1, :, 0:ny], w2[c, z + 1, 0:nx, :]
            total = (ahead(vx, 0) + behind(vx, 0))[0:nx] + (ahead(vy, 1) + behind(vy, 1))[:, 0:ny]
            total = total + (w2[c, z + 2, 0:nx, 0:ny] + w2[c, z, 0:nx, 0:ny])
            if c == 0:
                slope = (ahead(here_x, 0) - behind(here_x, 0))[0:nx]
            elif c == 1:
                slope = (ahead(here_y, 1) - behind(here_y, 1))[:, 0:ny]
            else:
                slope = div[z + 2, 0:nx, 0:ny] - div[z, 0:nx, 0:ny]
            third = own * v - 0.125 * total - (1.0 / 64.0) * slope
            res_ref[c, i] = third
            zeroth = d_now * fields[c, 0:nx, 0:ny]
            one = w1[c, z + 1, 0:nx, 0:ny]
            for k, term in enumerate(
                (zeroth * zeroth, zeroth * one, one * one, one * v, v * v, v * third)
            ):
                sums[k] = sums[k] + folded(term)
        return tuple(sums)

    sums = lax.fori_loop(0, nz, third_layer, tuple(jnp.zeros((8, ny), F32) for _ in range(MOMENTS)))

    lane = iota((1, ny), 1)
    message = part_ref[...]
    for k in range(MOMENTS):
        amount = jnp.sum(jnp.sum(sums[k], axis=0, keepdims=True), axis=1, keepdims=True)
        message = message + jnp.where(lane == k, amount, 0.0)
    row_out[0] = message
    slot = gy * 2 + gz
    row_in[slot] = message
    copies = []
    for k in range(1, ngy):
        copies.append((wrap(gy + k, ngy), gz))
    for k in range(ngy):
        copies.append((wrap(gy + k, ngy), other))
    started = []
    for k, (y, z) in enumerate(copies):
        copy = remote(row_out.at[0], row_in.at[slot], 15 + k, at(gx, y, z))
        copy.start()
        started.append(copy)
    for copy in started:
        copy.wait()
    message = row_in[0]
    for k in range(1, 2 * ngy):
        message = message + row_in[k]
    row_out[1] = message
    ring_in[gx] = message
    first_index = 15 + len(copies)
    started = []
    for k in range(1, ngx):
        copy = remote(row_out.at[1], ring_in.at[gx], first_index + k - 1, at(wrap(gx + k, ngx), gy, gz))
        copy.start()
        started.append(copy)
    for copy in started:
        copy.wait()
    message = ring_in[0]
    for k in range(1, ngx):
        message = message + ring_in[k]
    parts = [jnp.sum(jnp.where(lane == k, message, 0.0), axis=1, keepdims=True) for k in range(MOMENTS + 2)]

    scale = lax.rsqrt(parts[MOMENTS] / (EPOCHS * parts[MOMENTS + 1]) + EPS) * (1.0 / PRE)
    iterate, residual = conjugate(parts[0:MOMENTS])
    iterate = [scale * value for value in iterate]
    residual = [scale * value for value in residual]

    def finish(i, carry):
        z = nz * gz + i
        d_now = table[0, z, :, 0:ny]
        for c in range(3):
            zeroth = d_now * fields[c, 0:nx, 0:ny]
            one, two = w1[c, z + 1, 0:nx, 0:ny], w2[c, z + 1, 0:nx, 0:ny]
            third = res_ref[c, i]
            adj_ref[c, i] = iterate[0] * zeroth + iterate[1] * one + iterate[2] * two
            res_ref[c, i] = residual[0] * zeroth + residual[1] * one + residual[2] * two + residual[3] * third
        return carry

    lax.fori_loop(0, nz, finish, 0)


def project(resid, look_vector):
    return jnp.einsum("ec,nep->ncp", look_vector, resid, precision=HIGHEST).astype(jnp.bfloat16)


def per_device(
    observed,
    predicted,
    coherence_mask,
    block_count,
    block_owner,
    block_matrix_choice,
    block_patch,
    look_vector,
    interp_weights,
    depth_kernel,
    stiffness,
):
    blocks, _, pixels = observed.shape
    cells = PATCH_X * PATCH_Y
    ngx, ngy = lax.axis_size("gx"), lax.axis_size("gy")
    owners = ngx * ngy
    nz, nx, ny = stiffness.shape
    places = (nx // PATCH_X) * (ny // PATCH_Y)

    column = lax.broadcasted_iota(jnp.int32, (blocks, pixels), 1)
    valid = coherence_mask.astype(F32) * (column < block_count[:, None]).astype(F32)
    resid = (predicted - observed) * valid[:, None, :]
    lane = jnp.arange(ny)
    part = jnp.where(lane == MOMENTS, jnp.sum(resid * resid), 0.0) + jnp.where(
        lane == MOMENTS + 1, jnp.sum(valid), 0.0
    )

    owner = block_owner[:, 0]
    order = lax.broadcasted_iota(jnp.int32, (blocks, blocks), 0)
    before = lax.broadcasted_iota(jnp.int32, (blocks, blocks), 1)
    earlier = (owner[:, None] == owner[None, :]) & (before < order)
    rank = jnp.sum(earlier.astype(jnp.int32), axis=1)
    slot = owner * CAP + rank
    select = (lax.broadcasted_iota(jnp.int32, (blocks, owners * CAP), 1) == slot[:, None]).astype(F32)
    at_owner = (lax.broadcasted_iota(jnp.int32, (blocks, owners), 1) == owner[:, None]).astype(F32)
    at_lane = (lax.broadcasted_iota(jnp.int32, (blocks, CAP * places), 1) == (rank * places + block_patch)[:, None])
    choice = jnp.einsum("bo,bl->ol", at_owner, at_lane.astype(F32))

    coeffs = project(resid, look_vector)
    picked = jnp.take(interp_weights, block_matrix_choice, axis=0)
    sums = jnp.einsum("aow,awv->aov", coeffs, picked, preferred_element_type=F32)
    slots = jnp.einsum(
        "bos,bcp->ocsp", select.reshape(blocks, owners, CAP), sums, precision=HIGHEST
    )

    depth = jnp.broadcast_to((PRE * depth_kernel)[:, None], (nz, 2 * ny))
    rows, lanes = nx + 8, 2 * ny
    out = jax.ShapeDtypeStruct((3, nz, nx, ny), F32)
    vmem = pl.BlockSpec(memory_space=pltpu.VMEM)
    copies = 15 + (2 * ngy - 1) + (ngx - 1)
    return pl.pallas_call(
        kernel,
        out_shape=(out, out),
        in_specs=[vmem] * 5,
        out_specs=(vmem, vmem),
        scratch_shapes=[
            pltpu.VMEM((owners, 3, CAP, cells), F32),
            pltpu.VMEM((owners, 1, cells), F32),
            pltpu.VMEM((3, owners * CAP, cells), F32),
            pltpu.VMEM((owners * CAP, cells), F32),
            pltpu.VMEM((2, 3, nx, ny), F32),
            pltpu.VMEM((3, nx, ny), F32),
            pltpu.VMEM((6, 3, 8, ny), F32),
            pltpu.VMEM((2, 3, nx, ny), F32),
            pltpu.VMEM((2, nz, 8, ny), F32),
            pltpu.VMEM((nz, rows, ny), F32),
            pltpu.VMEM((2, 8, nz * rows), F32),
            pltpu.VMEM((2, 8, nz * rows), F32),
            pltpu.VMEM((2 * nz, rows, lanes), F32),
            pltpu.VMEM((2 * nz + 16, lanes), F32),
            pltpu.VMEM((5, 2 * nz, 1, lanes), F32),
            pltpu.VMEM((9, rows, lanes), F32),
            pltpu.VMEM((3, 2 * nz + 2, rows, lanes), F32),
            pltpu.VMEM((3, 2 * nz + 2, rows, lanes), F32),
            pltpu.VMEM((2 * nz + 2, rows, lanes), F32),
            pltpu.VMEM((2, 1, ny), F32),
            pltpu.VMEM((2 * ngy, 1, ny), F32),
            pltpu.VMEM((ngx, 1, ny), F32),
            pltpu.SemaphoreType.DMA((2,)),
            pltpu.SemaphoreType.DMA((2,)),
            pltpu.SemaphoreType.DMA((copies,)),
            pltpu.SemaphoreType.DMA((copies,)),
        ],
        compiler_params=pltpu.CompilerParams(
            collective_id=0, has_side_effects=True, vmem_limit_bytes=48 * 1024 * 1024
        ),
    )(slots, choice[:, None, :], part[None, :], depth, stiffness)


def solution(mesh):
    in_specs = (
        P(("grp", "gx", "gy", "gz"), None, None),
        P(("grp", "gx", "gy", "gz"), None, None),
        P(("grp", "gx", "gy", "gz"), None),
        P(("grp", "gx", "gy", "gz")),
        P(("grp", "gx", "gy", "gz"), None),
        P(("grp", "gx", "gy", "gz")),
        P(("grp", "gx", "gy", "gz")),
        P(),
        P(),
        P(("grp", "gz")),
        P(("grp", "gz"), "gx", "gy"),
    )
    out_specs = (P(None, ("grp", "gz"), "gx", "gy"), P(None, ("grp", "gz"), "gx", "gy"))
    return jax.shard_map(
        per_device, mesh=mesh, in_specs=in_specs, out_specs=out_specs, check_vma=False
    )
```

profile of v0, /device:TPU:33, one launch (start us, length us, event | category | flops | bytes accessed | tf_op | source)
XLA Modules:
  0.0 101.4 jit_solution(10402767048676751010)
XLA Ops:
  0.6 0.0 copy-start
  0.6 1.0 convert_reduce_fusion
  1.6 0.7 multiply_add_fusion.1
  2.3 0.7 fusion.21
  3.0 0.7 broadcast_multiply_fusion
  3.6 0.7 compare_and_fusion
  4.3 0.7 compare_select_fusion
  5.0 0.1 broadcast_in_dim.45.depth_ref
  5.0 0.9 fusion.16
  6.0 1.5 %fusion.23 = (f32[]{:T(128)}, f32[64,256]{1,0:T(8,128)S(1)}) fusion(s32[64,256]{1,0:T(8,128)} %param.13, s32[64]{0:T(128)} %param.14), kind=kLoop, calls=%fused_computation.41 | loop fusion | flops 65535 | bytes 131332 | tf_op jit(solution)/shard_map/reduce_sum | solution.py:474
  7.5 1.8 %multiply_reduce_fusion = f32[]{:T(128)} fusion(f32[64,256]{1,0:T(8,128)S(1)} %get-tuple-element.3, f32[64,4,256]{2,1,0:T(4,128)} %param.12, f32[64,4,256]{2,1,0:T(4,128)} %param.11), kind=kLoop, calls=%fused_computation.7 | loop fusion | flops 262143 | bytes 589828 | tf_op jit(solution)/shard_map/reduce_sum | solution.py:473
  9.3 1.3 %fusion.20.part_ref = f32[1,128]{1,0:T(1,128)S(1)} fusion(f32[]{:T(128)} %get-tuple-element.2, f32[]{:T(128)} %multiply_reduce_fusion), kind=kLoop, calls=%fused_computation.35 | loop fusion | flops 640 | bytes 520 | tf_op jit(solution)/shard_map/add | solution.py:473
  10.6 1.7 %fusion.14 = bf16[64,256,3]{1,2,0:T(4,128)(2,1)S(1)} fusion(f32[64,4,256]{2,1,0:T(4,128)} %param.12, f32[64,4,256]{2,1,0:T(4,128)} %param.11, f32[64,256]{1,0:T(8,128)S(1)} %get-tuple-element.3, f32[4,3]{1,0:T(4,128)} %param.18), kind=kOutput, calls=%fused_computation.19 | convolution fusion | flops 2490368 | bytes 688176 | tf_op jit(solution)/shard_map/ec,nep->ncp/dot_general | solution.py:446
  12.3 0.0 copy-done
  12.3 3.0 %gather_fusion = bf16[64,256,128]{2,1,0:T(8,128)(2,1)} fusion(bf16[32,256,128]{2,1,0:T(8,128)(2,1)S(1)} %copy-done, s32[1024]{0:T(1024)S(1)} %pad_clamp_fusion), kind=kCustom, calls=%fused_computation | custom fusion | bytes 8388864 | tf_op jit(solution)/shard_map/jit(_take)/gather | solution.py:489
  15.3 0.0 copy-start.1
  15.3 3.0 %fusion.4 = f32[64,3,128,1]{2,1,0,3:T(4,128)S(1)} fusion(bf16[64,256,128]{2,1,0:T(8,128)(2,1)} %gather_fusion, pred[64]{0:T(512)(128)(4,1)S(1)} %compare_and_fusion, bf16[64,256,3]{1,0,2:T(8,128)(2,1)S(1)} %copy.27), kind=kOutput, calls=%fused_computation.5 | convolution fusion | flops 14680064 | bytes 4390976 | tf_op jit(solution)/shard_map/aow,awv->aov/dot_general | solution.py:490
  18.3 0.4 fusion.8
  18.7 0.3 copy.28
  18.9 0.0 copy-done.1
  19.0 80.7 %shard_map.122 = (f32[3,16,32,128]{3,2,1,0:T(8,128)S(1)}, f32[3,16,32,128]{3,2,1,0:T(8,128)S(1)}) custom-call(f32[64,3,4,128]{3,2,1,0:T(4,128)S(1)} %bitcast.19, f32[64,1,128]{2,1,0:T(1,128)S(1)} %bitcast.20, f32[1,128]{1,0:T(1,128)S(1)} %fusion.20.part_ref, f32[16,256]{1,0:T(8,128)S(1)} %broadcast_in_dim.45.depth_ref, f32[16,32,128]{2,1,0:T(8,128)S(1)} %copy-done.1), custom_call_target="tpu_custom_call" | custom-call | tf_op jit(solution)/shard_map/pallas_call | solution.py:500
  99.7 0.9 copy.31
  100.6 0.9 copy.32
  (3 shorter events, 0.0 us)
Async XLA Ops:
  0.6 11.6 %copy-start = (bf16[32,256,128]{2,1,0:T(8,128)(2,1)S(1)}, bf16[32,256,128]{2,1,0:T(8,128)(2,1)}, u32[]{:S(2)}) copy-start(bf16[32,256,128]{2,1,0:T(8,128)(2,1)} %param.19) | copy-start | bytes 6291460
  15.3 3.7 %copy-start.1 = (f32[16,32,128]{2,1,0:T(8,128)S(1)}, f32[16,32,128]{2,1,0:T(8,128)}, u32[]{:S(2)}) copy-start(f32[16,32,128]{2,1,0:T(8,128)} %stiff_ref.1) | copy-start | bytes 786436
where the time goes:
time: 102 us; the launch traced here: 101 us
  Pallas kernels  80.7 us (79%)
  other arithmetic  8.92 us (9%)
  matrix products  5.96 us (6%)
  local copies, waits for them, and re-layouts  5.12 us (5%)
    pallas_call x1, Pallas kernels, per_device(): pl.pallas_call(kernel, out_shape=(out, out), in_specs=[vmem] * 5, out_spe...  80.7 us
    dot_general x1, matrix products, per_device(): jnp.einsum('aow,awv->aov', coeffs, picked, preferred_element_type=F32)  3.01 us
    gather x1, local copies, waits for them, and re-layouts, per_device(): picked = jnp.take(interp_weights, block_matrix_choice, axis=0)  3.01 us

commit v1 on v0

--- a/solution.py
+++ b/solution.py
@@ -85,16 +85,28 @@
 
 
 def kernel(
-    slots_ref, choice_ref, part_ref, depth_ref, stiff_ref,
+    observed_hbm, predicted_hbm, coherence_hbm, count_hbm, owner_hbm, table_hbm, patch_hbm, look_hbm,
+    weights_hbm, depth_hbm, stiff_hbm,
     adj_ref, res_ref,
+    observed_ref, predicted_ref, coherence_ref, count_ref, owner_ref, table_ref, patch_ref, look_ref,
+    weights, depth_ref, stiff_ref,
+    numbers, valid, resid, coeffs, slots_ref, choice_ref,
     got_slots, got_choice, flat_slots, flat_choice,
     surf, surf_other, halo_x, halo_y,
     stiff_x, wide_stiff, strip_out, strip_in, coef,
     depths, table,
     fields, w1, w2, div,
     row_out, row_in, ring_in,
-    send_a2a, recv_a2a, send_sem, recv_sem,
+    send_a2a, recv_a2a, send_sem, recv_sem, local_sem,
 ):
+    pairs = (
+        (depth_hbm, depth_ref), (count_hbm, count_ref), (owner_hbm, owner_ref), (table_hbm, table_ref),
+        (patch_hbm, patch_ref), (look_hbm, look_ref), (coherence_hbm, coherence_ref),
+        (predicted_hbm, predicted_ref), (observed_hbm, observed_ref), (weights_hbm, weights), (stiff_hbm, stiff_ref),
+    )
+    fetches = [pltpu.make_async_copy(a, b, local_sem.at[i]) for i, (a, b) in enumerate(pairs)]
+    for fetch in fetches:
+        fetch.start()
     gx, gy, gz = lax.axis_index("gx"), lax.axis_index("gy"), lax.axis_index("gz")
     ngx, ngy = lax.axis_size("gx"), lax.axis_size("gy")
     owners = ngx * ngy
@@ -111,7 +123,13 @@
         return lax.rem(value + count, count)
 
     depths[...] = jnp.zeros(depths.shape, F32)
-    depths[pl.ds(pl.multiple_of(8 + nz * gz, 8), nz), :] = depth_ref[...]
+    own_layers = pl.ds(pl.multiple_of(8 + nz * gz, 8), nz)
+    fetches[0].wait()
+    layer = iota((nz, lanes), 0)
+    own_depths = jnp.zeros((nz, lanes), F32)
+    for z in range(nz):
+        own_depths = jnp.where(layer == z, PRE * depth_ref[z], own_depths)
+    depths[own_layers, :] = own_depths
 
     barrier = pltpu.get_barrier_semaphore()
 
@@ -137,6 +155,60 @@
         for c in range(3):
             w1[c, edge] = zero_plane
             w2[c, edge] = zero_plane
+    blocks, epochs, pixels = observed_ref.shape
+    for fetch in fetches[1:9]:
+        fetch.wait()
+    for b in range(blocks):
+        for k, source in enumerate((count_ref, table_ref, patch_ref, owner_ref)):
+            numbers[k, b:b + 1, :] = jnp.full((1, ny), source[b], jnp.int32)
+    in_scene = iota((blocks, ny), 1)
+    for k in range(0, pixels, ny):
+        kept = (in_scene + k < numbers[0]).astype(F32)
+        valid[:, k:k + ny] = coherence_ref[:, k:k + ny].astype(F32) * kept
+    for b in range(blocks):
+        resid[epochs * b:epochs * (b + 1), :] = (predicted_ref[b] - observed_ref[b]) * valid[b:b + 1, :]
+    res = resid[...]
+    row_block, row_place = iota((blocks, epochs * blocks), 0), iota((blocks, epochs * blocks), 1)
+    own_rows = row_place // epochs == row_block
+    for c in range(3):
+        mix = jnp.zeros((blocks, epochs * blocks), F32)
+        for e in range(epochs):
+            mix = jnp.where(own_rows & (row_place % epochs == e), look_ref[e, c], mix)
+        coeffs[c * blocks:(c + 1) * blocks, :] = jnp.dot(
+            mix, res, precision=HIGHEST, preferred_element_type=F32
+        )
+    mass = jnp.sum(jnp.sum(res * res, axis=0, keepdims=True), axis=1, keepdims=True)
+    weight = jnp.sum(jnp.sum(valid[...], axis=0, keepdims=True), axis=1, keepdims=True)
+
+    lane_owner = iota((blocks, owners), 1)
+    at_owner = (lane_owner == numbers[3, :, 0:owners]).astype(F32)
+    before = (iota((blocks, blocks), 1) < iota((blocks, blocks), 0)).astype(F32)
+    ahead_of = jnp.dot(before, at_owner, preferred_element_type=F32)
+    rank = jnp.sum(ahead_of * at_owner, axis=1, keepdims=True).astype(jnp.int32)
+    slot_of = numbers[3, :, 0:1] * CAP + rank
+    select = (iota((blocks, owners * CAP), 1) == slot_of).astype(F32)
+    at_lane = (iota((blocks, ny), 1) == rank * (ny // CAP) + numbers[2]).astype(F32)
+    marks = lax.dot_general(at_owner, at_lane, (((0,), (0,)), ((), ())), preferred_element_type=F32)
+    for o in range(owners):
+        choice_ref[o] = marks[o:o + 1]
+
+    rounded = coeffs[...].astype(jnp.bfloat16).astype(F32)
+    which = jnp.concatenate([numbers[1]] * 3, axis=0)
+    which = jnp.concatenate([which] * (pixels // ny), axis=1)
+    fetches[9].wait()
+    total_sums = jnp.zeros((3 * blocks, ny), F32)
+    for t in range(weights.shape[0]):
+        taken = jnp.where(which == t, rounded, 0.0).astype(jnp.bfloat16)
+        total_sums = total_sums + jnp.dot(taken, weights[t], preferred_element_type=F32)
+    for c in range(3):
+        chosen = lax.dot_general(
+            select, total_sums[c * blocks:(c + 1) * blocks], (((0,), (0,)), ((), ())),
+            precision=HIGHEST, preferred_element_type=F32,
+        )
+        for o in range(owners):
+            slots_ref[o, c] = chosen[CAP * o:CAP * (o + 1)]
+
+    fetches[10].wait()
     pl.semaphore_wait(barrier, owners - 1 + ngy)
 
     def remote(source, target, index, device):
@@ -147,11 +219,10 @@
 
     x_up, x_down = wrap(gx + 1, ngx), wrap(gx - 1, ngx)
     y_up, y_down = wrap(gy + 1, ngy), wrap(gy - 1, ngy)
-    own_depth = depth_ref
     early = [
         remote(stiff_ref.at[:, pl.ds(0, 8), :], stiff_x.at[0], 0, at(x_down, gy, gz)),
         remote(stiff_ref.at[:, pl.ds(nx - 8, 8), :], stiff_x.at[1], 1, at(x_up, gy, gz)),
-        remote(own_depth, depths.at[pl.ds(pl.multiple_of(8 + nz * gz, 8), nz), :], 2, at(gx, gy, other)),
+        remote(depths.at[own_layers, :], depths.at[own_layers, :], 2, at(gx, gy, other)),
     ]
     for copy in early:
         copy.start()
@@ -386,7 +457,7 @@
     sums = lax.fori_loop(0, nz, third_layer, tuple(jnp.zeros((8, ny), F32) for _ in range(MOMENTS)))
 
     lane = iota((1, ny), 1)
-    message = part_ref[...]
+    message = jnp.where(lane == MOMENTS, mass, 0.0) + jnp.where(lane == MOMENTS + 1, weight, 0.0)
     for k in range(MOMENTS):
         amount = jnp.sum(jnp.sum(sums[k], axis=0, keepdims=True), axis=1, keepdims=True)
         message = message + jnp.where(lane == k, amount, 0.0)
@@ -442,10 +513,6 @@
     lax.fori_loop(0, nz, finish, 0)
 
 
-def project(resid, look_vector):
-    return jnp.einsum("ec,nep->ncp", look_vector, resid, precision=HIGHEST).astype(jnp.bfloat16)
-
-
 def per_device(
     observed,
     predicted,
@@ -459,50 +526,40 @@
     depth_kernel,
     stiffness,
 ):
-    blocks, _, pixels = observed.shape
+    blocks, epochs, pixels = observed.shape
     cells = PATCH_X * PATCH_Y
     ngx, ngy = lax.axis_size("gx"), lax.axis_size("gy")
     owners = ngx * ngy
     nz, nx, ny = stiffness.shape
-    places = (nx // PATCH_X) * (ny // PATCH_Y)
-
-    column = lax.broadcasted_iota(jnp.int32, (blocks, pixels), 1)
-    valid = coherence_mask.astype(F32) * (column < block_count[:, None]).astype(F32)
-    resid = (predicted - observed) * valid[:, None, :]
-    lane = jnp.arange(ny)
-    part = jnp.where(lane == MOMENTS, jnp.sum(resid * resid), 0.0) + jnp.where(
-        lane == MOMENTS + 1, jnp.sum(valid), 0.0
-    )
-
-    owner = block_owner[:, 0]
-    order = lax.broadcasted_iota(jnp.int32, (blocks, blocks), 0)
-    before = lax.broadcasted_iota(jnp.int32, (blocks, blocks), 1)
-    earlier = (owner[:, None] == owner[None, :]) & (before < order)
-    rank = jnp.sum(earlier.astype(jnp.int32), axis=1)
-    slot = owner * CAP + rank
-    select = (lax.broadcasted_iota(jnp.int32, (blocks, owners * CAP), 1) == slot[:, None]).astype(F32)
-    at_owner = (lax.broadcasted_iota(jnp.int32, (blocks, owners), 1) == owner[:, None]).astype(F32)
-    at_lane = (lax.broadcasted_iota(jnp.int32, (blocks, CAP * places), 1) == (rank * places + block_patch)[:, None])
-    choice = jnp.einsum("bo,bl->ol", at_owner, at_lane.astype(F32))
-
-    coeffs = project(resid, look_vector)
-    picked = jnp.take(interp_weights, block_matrix_choice, axis=0)
-    sums = jnp.einsum("aow,awv->aov", coeffs, picked, preferred_element_type=F32)
-    slots = jnp.einsum(
-        "bos,bcp->ocsp", select.reshape(blocks, owners, CAP), sums, precision=HIGHEST
-    )
-
-    depth = jnp.broadcast_to((PRE * depth_kernel)[:, None], (nz, 2 * ny))
+
     rows, lanes = nx + 8, 2 * ny
     out = jax.ShapeDtypeStruct((3, nz, nx, ny), F32)
     vmem = pl.BlockSpec(memory_space=pltpu.VMEM)
+    far = pl.BlockSpec(memory_space=pltpu.HBM)
     copies = 15 + (2 * ngy - 1) + (ngx - 1)
     return pl.pallas_call(
         kernel,
         out_shape=(out, out),
-        in_specs=[vmem] * 5,
+        in_specs=[far] * 11,
         out_specs=(vmem, vmem),
         scratch_shapes=[
+            pltpu.VMEM(observed.shape, F32),
+            pltpu.VMEM(predicted.shape, F32),
+            pltpu.VMEM(coherence_mask.shape, jnp.int32),
+            pltpu.SMEM((blocks,), jnp.int32),
+            pltpu.SMEM((blocks,), jnp.int32),
+            pltpu.SMEM((blocks,), jnp.int32),
+            pltpu.SMEM((blocks,), jnp.int32),
+            pltpu.SMEM(look_vector.shape, F32),
+            pltpu.VMEM(interp_weights.shape, interp_weights.dtype),
+            pltpu.SMEM((nz,), F32),
+            pltpu.VMEM(stiffness.shape, F32),
+            pltpu.VMEM((4, blocks, ny), jnp.int32),
+            pltpu.VMEM((blocks, pixels), F32),
+            pltpu.VMEM((epochs * blocks, pixels), F32),
+            pltpu.VMEM((3 * blocks, pixels), F32),
+            pltpu.VMEM((owners, 3, CAP, cells), F32),
+            pltpu.VMEM((owners, 1, cells), F32),
             pltpu.VMEM((owners, 3, CAP, cells), F32),
             pltpu.VMEM((owners, 1, cells), F32),
             pltpu.VMEM((3, owners * CAP, cells), F32),
@@ -529,11 +586,15 @@
             pltpu.SemaphoreType.DMA((2,)),
             pltpu.SemaphoreType.DMA((copies,)),
             pltpu.SemaphoreType.DMA((copies,)),
+            pltpu.SemaphoreType.DMA((11,)),
         ],
         compiler_params=pltpu.CompilerParams(
-            collective_id=0, has_side_effects=True, vmem_limit_bytes=48 * 1024 * 1024
+            collective_id=0, has_side_effects=True, vmem_limit_bytes=67043328
         ),
-    )(slots, choice[:, None, :], part[None, :], depth, stiffness)
+    )(
+        observed, predicted, coherence_mask, block_count, block_owner[:, 0], block_matrix_choice, block_patch,
+        look_vector, interp_weights, depth_kernel, stiffness,
+    )
 
 
 def solution(mesh):

time: 102 us -> 86.7 us (0.85)
  other arithmetic: 8.92 us -> 0 us
  matrix products: 5.96 us -> 0 us
  local copies, waits for them, and re-layouts: 5.12 us -> 3.02 us
  Pallas kernels: 80.7 us -> 82.7 us
    dot_general x4 -> x0, matrix products: 5.96 us -> none  [the longest x1 3.01 us: per_device(): jnp.einsum('aow,awv->aov', coeffs, picked, preferred_element_type=F32)]
    reduce_sum x3 -> x0, other arithmetic: 4.32 us -> none  [the longest x1 1.78 us: per_device(): jnp.sum(resid * resid)]
    gather x1 -> x0, local copies, waits for them, and re-layouts: 3.01 us -> none  [per_device(): picked = jnp.take(interp_weights, block_matrix_choice, axis=0)]
    pallas_call x1, Pallas kernels: 80.7 us -> 82.7 us  [per_device(): pl.pallas_call(kernel, out_shape=(out, out), in_specs=[far] * 11, out_spe...]
    add x2 -> x0, other arithmetic: 1.96 us -> none  [the longest x1 1.3 us: per_device(): jnp.where(lane == MOMENTS, jnp.sum(resid * resid), 0.0)]
    unnamed x6 -> x4, local copies, waits for them, and re-layouts: 1.77 us -> 3.02 us
where the time goes in v1:
time: 86.7 us; the launch traced here: 86.4 us
  Pallas kernels  82.7 us (95%)
  local copies, waits for them, and re-layouts  3.02 us (3%)
    pallas_call x1, Pallas kernels, per_device(): pl.pallas_call(kernel, out_shape=(out, out), in_specs=[far] * 11, out_spe...  82.7 us
    unnamed x4, local copies, waits for them, and re-layouts  3.02 us

profile of v1, /device:TPU:33, one launch (start us, length us, event | category | flops | bytes accessed | tf_op | source)
XLA Modules:
  0.0 86.4 jit_solution(17753783261551550315)
XLA Ops:
  0.6 82.7 %shard_map.122 = (f32[3,16,32,128]{3,2,1,0:T(8,128)}, f32[3,16,32,128]{3,2,1,0:T(8,128)}) custom-call(f32[64,4,256]{2,1,0:T(4,128)} %observed_hbm.1, f32[64,4,256]{2,1,0:T(4,128)} %predicted_hbm.1, s32[64,256]{1,0:T(8,128)} %coherence_hbm.1, s32[64]{0:T(128)} %count_hbm.1, s32[64]{0:T(128)} %bitcast.1, s32[64]{0:T(128)} %table_hbm.1, s32[64]{0:T(128)} %patch_hbm.1, ...), custom_call_target="tpu_custom_call" | custom-call | tf_op jit(solution)/shard_map/pallas_call | solution.py:540
  83.4 0.0 copy-start
  83.4 2.1 %copy.15 = f32[3,16,32,128]{3,2,1,0:T(8,128)} copy(f32[3,16,32,128]{3,2,1,0:T(8,128)} %get-tuple-element.4) | data formatting | bytes 1572864
  85.5 0.0 copy-done
  85.5 0.9 %copy.16 = f32[3,16,32,128]{3,2,1,0:T(8,128)} copy(f32[3,16,32,128]{3,2,1,0:T(8,128)S(1)} %copy-done) | data formatting | bytes 1572864
Async XLA Ops:
  83.4 2.1 %copy-start = (f32[3,16,32,128]{3,2,1,0:T(8,128)S(1)}, f32[3,16,32,128]{3,2,1,0:T(8,128)}, u32[]{:S(2)}) copy-start(f32[3,16,32,128]{3,2,1,0:T(8,128)} %get-tuple-element.5) | copy-start | bytes 2359300

commit v2 on v1

--- a/solution.py
+++ b/solution.py
@@ -92,12 +92,12 @@
     weights, depth_ref, stiff_ref,
     numbers, valid, resid, coeffs, slots_ref, choice_ref,
     got_slots, got_choice, flat_slots, flat_choice,
-    surf, surf_other, halo_x, halo_y,
+    surf, surf_other, border, halo_x, halo_y,
     stiff_x, wide_stiff, strip_out, strip_in, coef,
     depths, table,
     fields, w1, w2, div,
     row_out, row_in, ring_in,
-    send_a2a, recv_a2a, send_sem, recv_sem, local_sem,
+    send_a2a, recv_a2a, send_sem, recv_sem, local_sem, chain, entered,
 ):
     pairs = (
         (depth_hbm, depth_ref), (count_hbm, count_ref), (owner_hbm, owner_ref), (table_hbm, table_ref),
@@ -130,17 +130,21 @@
     for z in range(nz):
         own_depths = jnp.where(layer == z, PRE * depth_ref[z], own_depths)
     depths[own_layers, :] = own_depths
+    stiff_x[...] = jnp.zeros(stiff_x.shape, F32)
 
     barrier = pltpu.get_barrier_semaphore()
-
-    def greet(k, carry):
-        o = lax.rem(me + k, owners)
-        pl.semaphore_signal(barrier, inc=1, device_id=at(o // ngy, lax.rem(o, ngy), gz))
-        return carry
-
-    lax.fori_loop(1, owners, greet, 0)
-    for k in range(ngy):
-        pl.semaphore_signal(barrier, inc=1, device_id=at(gx, wrap(gy + k, ngy), other))
+    peers = [(wrap(gy + k, ngy), gz) for k in range(1, ngy)] + [(wrap(gy + k, ngy), other) for k in range(ngy)]
+    below, above = gx > 0, gx < ngx - 1
+    for y, z in peers:
+        pl.semaphore_signal(barrier, inc=1, device_id=at(gx, y, z))
+
+    @pl.when(below)
+    def _():
+        pl.semaphore_signal(barrier, inc=1, device_id=at(gx - 1, gy, gz))
+
+    @pl.when(above)
+    def _():
+        pl.semaphore_signal(barrier, inc=1, device_id=at(gx + 1, gy, gz))
 
     def domain(count):
         r, c = iota((count, lanes), 0), iota((count, lanes), 1)
@@ -158,6 +162,23 @@
     blocks, epochs, pixels = observed_ref.shape
     for fetch in fetches[1:9]:
         fetch.wait()
+
+    pl.semaphore_wait(barrier, len(peers) + below.astype(jnp.int32) + above.astype(jnp.int32))
+
+    @pl.when(below)
+    def _():
+        pl.semaphore_wait(chain, 1)
+
+    @pl.when(above)
+    def _():
+        pl.semaphore_signal(chain, inc=1, device_id=at(gx + 1, gy, gz))
+
+    def announce(j, carry):
+        pl.semaphore_signal(entered.at[gx], inc=1, device_id=at(j, gy, gz))
+        return carry
+
+    lax.fori_loop(0, gx, announce, 0)
+
     for b in range(blocks):
         for k, source in enumerate((count_ref, table_ref, patch_ref, owner_ref)):
             numbers[k, b:b + 1, :] = jnp.full((1, ny), source[b], jnp.int32)
@@ -209,43 +230,71 @@
             slots_ref[o, c] = chosen[CAP * o:CAP * (o + 1)]
 
     fetches[10].wait()
-    pl.semaphore_wait(barrier, owners - 1 + ngy)
-
-    def remote(source, target, index, device):
+
+    def remote(source, target, index, device, arrival=None):
         return pltpu.make_async_remote_copy(
-            src_ref=source, dst_ref=target, send_sem=send_sem.at[index], recv_sem=recv_sem.at[index],
+            src_ref=source, dst_ref=target, send_sem=send_sem.at[index],
+            recv_sem=recv_sem.at[index if arrival is None else arrival],
             device_id=device, device_id_type=pl.DeviceIdType.MESH,
         )
 
+    def post(j, first):
+        for k in range(first, ngy):
+            y = wrap(gy + k, ngy)
+            o = j * ngy + y
+            for message, (source, target) in enumerate(((slots_ref, got_slots), (choice_ref, got_choice))):
+                pltpu.make_async_remote_copy(
+                    src_ref=source.at[o], dst_ref=target.at[me],
+                    send_sem=send_a2a.at[message], recv_sem=recv_a2a.at[message],
+                    device_id=at(j, y, gz), device_id_type=pl.DeviceIdType.MESH,
+                ).start()
+
+    def post_known(i, carry):
+        d = ngx // 2 - i
+        down, up = wrap(gx - d, ngx), wrap(gx + d, ngx)
+
+        @pl.when(down < gx)
+        def _():
+            post(down, 0)
+
+        @pl.when((up < gx) & (d < ngx // 2))
+        def _():
+            post(up, 0)
+
+        return carry
+
+    lax.fori_loop(0, ngx // 2, post_known, 0)
+    post(gx, 1)
+
     x_up, x_down = wrap(gx + 1, ngx), wrap(gx - 1, ngx)
     y_up, y_down = wrap(gy + 1, ngy), wrap(gy - 1, ngy)
-    early = [
-        remote(stiff_ref.at[:, pl.ds(0, 8), :], stiff_x.at[0], 0, at(x_down, gy, gz)),
-        remote(stiff_ref.at[:, pl.ds(nx - 8, 8), :], stiff_x.at[1], 1, at(x_up, gy, gz)),
-        remote(depths.at[own_layers, :], depths.at[own_layers, :], 2, at(gx, gy, other)),
-    ]
-    for copy in early:
-        copy.start()
-
-    def post(k, carry):
-        o = lax.rem(me + k, owners)
-        device = at(o // ngy, lax.rem(o, ngy), gz)
-        pltpu.make_async_remote_copy(
-            src_ref=slots_ref.at[o], dst_ref=got_slots.at[me], send_sem=send_a2a.at[0], recv_sem=recv_a2a.at[0],
-            device_id=device, device_id_type=pl.DeviceIdType.MESH,
-        ).start()
-        pltpu.make_async_remote_copy(
-            src_ref=choice_ref.at[o], dst_ref=got_choice.at[me], send_sem=send_a2a.at[1], recv_sem=recv_a2a.at[1],
-            device_id=device, device_id_type=pl.DeviceIdType.MESH,
-        ).start()
-        return carry
-
-    lax.fori_loop(1, owners, post, 0)
+    to_down = remote(stiff_ref.at[:, pl.ds(0, 8), :], stiff_x.at[0], 0, at(x_down, gy, gz))
+    to_up = remote(stiff_ref.at[:, pl.ds(nx - 8, 8), :], stiff_x.at[1], 1, at(x_up, gy, gz))
+    to_other = remote(depths.at[own_layers, :], depths.at[own_layers, :], 2, at(gx, gy, other))
+    to_other.start()
+
+    @pl.when(below)
+    def _():
+        to_down.start()
+
+    @pl.when(above)
+    def _():
+        to_up.start()
+
     got_slots[me] = slots_ref[me]
     got_choice[me] = choice_ref[me]
 
-    for copy in early:
-        copy.wait()
+    @pl.when(below)
+    def _():
+        to_down.wait_send()
+        to_up.wait_recv()
+
+    @pl.when(above)
+    def _():
+        to_up.wait_send()
+        to_down.wait_recv()
+
+    to_other.wait()
     low = iota((8, ny), 0) < 4
     for z in range(nz):
         wide_stiff[z, 0:nx, :] = stiff_ref[z]
@@ -288,6 +337,13 @@
     passed = pl.ds((nz - 4) + 4 * gz, 4)
     layers = remote(coef.at[passed], coef.at[passed], 5, at(gx, gy, other))
     layers.start()
+
+    def post_later(j, carry):
+        pl.semaphore_wait(entered.at[j], 1)
+        post(j, 0)
+        return carry
+
+    lax.fori_loop(gx + 1, ngx, post_later, 0)
 
     for message, buffer in enumerate((slots_ref, choice_ref)):
         part = buffer.at[pl.ds(0, owners - 1)]
@@ -319,31 +375,40 @@
         from_below = roll(roll(tile, -bit, 0), bit * PATCH_Y, 1)
         from_above = roll(roll(tile, bit, 0), -bit * PATCH_Y, 1)
         tile = jnp.where(row_set == chunk_set, tile, jnp.where(row_set, from_above, from_below))
-    surf[0] = tile.reshape(3, nx, ny)
-    swap = remote(surf.at[0], surf_other, 6, at(gx, gy, other))
+    surf[...] = tile.reshape(3, nx, ny)
+    turned = tile.T
+    border[0] = turned[0:8]
+    border[1] = turned[ny - 8:ny]
+
+    swap = remote(surf, surf_other, 6, at(gx, gy, other))
     swap.start()
+    first, last = pl.ds(0, 8), pl.ds(nx - 8, 8)
+    ways = (
+        (surf.at[:, first, :], halo_x, 0, x_down, gy),
+        (surf.at[:, last, :], halo_x, 1, x_up, gy),
+        (border.at[0], halo_y, 0, gx, y_down),
+        (border.at[1], halo_y, 1, gx, y_up),
+        (border.at[0], halo_y, 2, x_down, y_down),
+        (border.at[1], halo_y, 3, x_down, y_up),
+        (border.at[0], halo_y, 4, x_up, y_down),
+        (border.at[1], halo_y, 5, x_up, y_up),
+    )
+    count = len(ways)
+    started = []
+    for k in reversed(range(count)):
+        source, target, place, x, y = ways[k]
+        for i, z in enumerate((gz, other)):
+            copy = remote(source, target.at[gz, place], 7 + i * count + k, at(x, y, z), 7 + gz * count + k)
+            copy.start()
+            started.append(copy)
     swap.wait()
-    surf[1] = surf[0] + surf_other[...]
-
-    first, last = pl.ds(0, 8), pl.ds(nx - 8, 8)
-    whole = surf.at[1]
-    halos = [
-        remote(whole.at[:, first, :], halo_x.at[0], 7, at(x_down, gy, gz)),
-        remote(whole.at[:, last, :], halo_x.at[1], 8, at(x_up, gy, gz)),
-        remote(whole.at[:, first, :], halo_x.at[2], 9, at(x_down, y_down, gz)),
-        remote(whole.at[:, first, :], halo_x.at[3], 10, at(x_down, y_up, gz)),
-        remote(whole.at[:, last, :], halo_x.at[4], 11, at(x_up, y_down, gz)),
-        remote(whole.at[:, last, :], halo_x.at[5], 12, at(x_up, y_up, gz)),
-        remote(whole, halo_y.at[0], 13, at(gx, y_down, gz)),
-        remote(whole, halo_y.at[1], 14, at(gx, y_up, gz)),
-    ]
-    for copy in halos:
-        copy.start()
-    for copy in halos:
-        copy.wait()
+    for k, (source, target, place, x, y) in enumerate(ways):
+        for i in range(2):
+            remote(source, target.at[i, place], 7 + i * count + k, at(x, y, gz)).wait_recv()
+    for copy in started:
+        copy.wait_send()
     mask_tall = domain(tall)
     mask = domain(rows)
-    left = iota((1, ny), 1) < ny // 2
     low_rows = iota((8, lanes), 0) < 4
 
     def packed(values):
@@ -351,17 +416,19 @@
             [values[0:nx], jnp.where(low_rows, values[nx:nx + 8], values[nx + 8:nx + 16])], axis=0
         )
 
+    blank = jnp.zeros((ny - 16, 3 * nx), F32)
+
+    def columns_of(place):
+        low_side, high_side = halo_y[0, place] + halo_y[1, place], halo_y[0, place + 1] + halo_y[1, place + 1]
+        return jnp.concatenate([low_side, blank, high_side], axis=0).T.reshape(3, nx, ny)
+
+    near, upper, lower = columns_of(0), columns_of(2), columns_of(4)
     around = []
     for c in range(3):
-        main = jnp.concatenate([surf[1, c], halo_x[0, c], halo_x[1, c]], axis=0)
-        side = jnp.concatenate(
-            [
-                jnp.where(left, halo_y[0, c], halo_y[1, c]),
-                jnp.where(left, halo_x[2, c], halo_x[3, c]),
-                jnp.where(left, halo_x[4, c], halo_x[5, c]),
-            ],
-            axis=0,
+        main = jnp.concatenate(
+            [surf[c] + surf_other[c], halo_x[0, 0, c] + halo_x[1, 0, c], halo_x[0, 1, c] + halo_x[1, 1, c]], axis=0
         )
+        side = jnp.concatenate([near[c], upper[c, 0:8], lower[c, nx - 8:nx]], axis=0)
         around.append(mask_tall * jnp.concatenate([main, side], axis=1))
     flux = mask_tall * (
         0.5 * ((ahead(around[0], 0) - behind(around[0], 0)) + (ahead(around[1], 1) - behind(around[1], 1)))
@@ -427,12 +494,31 @@
             total = total + values[k:k + 8]
         return total
 
-    def third_layer(i, sums):
+    def gather_moments(i, sums):
+        z = nz * gz + i
+        own = coef[z, 0:nx, 0:ny]
+        d_now = table[0, z, :, 0:ny]
+        here = div[z + 1, 0:nx, 0:ny]
+        terms = [None] * MOMENTS
+        terms[MOMENTS - 1] = (1.0 / 64.0) * (here * here)
+        for c in range(3):
+            v = w2[c, z + 1, 0:nx, 0:ny]
+            total = ahead(w2[c, z + 1, :, 0:ny], 0)[0:nx] + ahead(w2[c, z + 1, 0:nx, :], 1)[:, 0:ny]
+            total = total + w2[c, z + 2, 0:nx, 0:ny]
+            zeroth = d_now * fields[c, 0:nx, 0:ny]
+            one = w1[c, z + 1, 0:nx, 0:ny]
+            for k, term in enumerate(
+                (zeroth * zeroth, zeroth * one, one * one, one * v, v * v, v * (own * v - 0.25 * total))
+            ):
+                terms[k] = term if terms[k] is None else terms[k] + term
+        return tuple(s + folded(t) for s, t in zip(sums, terms))
+
+    sums = lax.fori_loop(0, nz, gather_moments, tuple(jnp.zeros((8, ny), F32) for _ in range(MOMENTS)))
+
+    def third_layer(i, carry):
         z = nz * gz + i
         own = coef[z, 0:nx, 0:ny]
         here_x, here_y = div[z + 1, :, 0:ny], div[z + 1, 0:nx, :]
-        d_now = table[0, z, :, 0:ny]
-        sums = list(sums)
         for c in range(3):
             v = w2[c, z + 1, 0:nx, 0:ny]
             vx, vy = w2[c, z + 1, :, 0:ny], w2[c, z + 1, 0:nx, :]
@@ -444,17 +530,10 @@
                 slope = (ahead(here_y, 1) - behind(here_y, 1))[:, 0:ny]
             else:
                 slope = div[z + 2, 0:nx, 0:ny] - div[z, 0:nx, 0:ny]
-            third = own * v - 0.125 * total - (1.0 / 64.0) * slope
-            res_ref[c, i] = third
-            zeroth = d_now * fields[c, 0:nx, 0:ny]
-            one = w1[c, z + 1, 0:nx, 0:ny]
-            for k, term in enumerate(
-                (zeroth * zeroth, zeroth * one, one * one, one * v, v * v, v * third)
-            ):
-                sums[k] = sums[k] + folded(term)
-        return tuple(sums)
-
-    sums = lax.fori_loop(0, nz, third_layer, tuple(jnp.zeros((8, ny), F32) for _ in range(MOMENTS)))
+            res_ref[c, i] = own * v - 0.125 * total - (1.0 / 64.0) * slope
+        return carry
+
+    early_layers = (3 * nz) // 8
 
     lane = iota((1, ny), 1)
     message = jnp.where(lane == MOMENTS, mass, 0.0) + jnp.where(lane == MOMENTS + 1, weight, 0.0)
@@ -464,16 +543,13 @@
     row_out[0] = message
     slot = gy * 2 + gz
     row_in[slot] = message
-    copies = []
-    for k in range(1, ngy):
-        copies.append((wrap(gy + k, ngy), gz))
-    for k in range(ngy):
-        copies.append((wrap(gy + k, ngy), other))
+    base = 7 + 2 * count
     started = []
-    for k, (y, z) in enumerate(copies):
-        copy = remote(row_out.at[0], row_in.at[slot], 15 + k, at(gx, y, z))
+    for k, (y, z) in enumerate(peers):
+        copy = remote(row_out.at[0], row_in.at[slot], base + k, at(gx, y, z))
         copy.start()
         started.append(copy)
+    lax.fori_loop(0, early_layers, third_layer, 0)
     for copy in started:
         copy.wait()
     message = row_in[0]
@@ -481,12 +557,13 @@
         message = message + row_in[k]
     row_out[1] = message
     ring_in[gx] = message
-    first_index = 15 + len(copies)
+    first_index = base + len(peers)
     started = []
     for k in range(1, ngx):
         copy = remote(row_out.at[1], ring_in.at[gx], first_index + k - 1, at(wrap(gx + k, ngx), gy, gz))
         copy.start()
         started.append(copy)
+    lax.fori_loop(early_layers, nz, third_layer, 0)
     for copy in started:
         copy.wait()
     message = ring_in[0]
@@ -533,10 +610,10 @@
     nz, nx, ny = stiffness.shape
 
     rows, lanes = nx + 8, 2 * ny
-    out = jax.ShapeDtypeStruct((3, nz, nx, ny), F32)
+    out = pltpu.VMEM((3, nz, nx, ny), F32)
     vmem = pl.BlockSpec(memory_space=pltpu.VMEM)
     far = pl.BlockSpec(memory_space=pltpu.HBM)
-    copies = 15 + (2 * ngy - 1) + (ngx - 1)
+    copies = 23 + (2 * ngy - 1) + (ngx - 1)
     return pl.pallas_call(
         kernel,
         out_shape=(out, out),
@@ -564,10 +641,11 @@
             pltpu.VMEM((owners, 1, cells), F32),
             pltpu.VMEM((3, owners * CAP, cells), F32),
             pltpu.VMEM((owners * CAP, cells), F32),
-            pltpu.VMEM((2, 3, nx, ny), F32),
             pltpu.VMEM((3, nx, ny), F32),
-            pltpu.VMEM((6, 3, 8, ny), F32),
-            pltpu.VMEM((2, 3, nx, ny), F32),
+            pltpu.VMEM((3, nx, ny), F32),
+            pltpu.VMEM((2, 8, 3 * nx), F32),
+            pltpu.VMEM((2, 2, 3, 8, ny), F32),
+            pltpu.VMEM((2, 6, 8, 3 * nx), F32),
             pltpu.VMEM((2, nz, 8, ny), F32),
             pltpu.VMEM((nz, rows, ny), F32),
             pltpu.VMEM((2, 8, nz * rows), F32),
@@ -587,9 +665,11 @@
             pltpu.SemaphoreType.DMA((copies,)),
             pltpu.SemaphoreType.DMA((copies,)),
             pltpu.SemaphoreType.DMA((11,)),
+            pltpu.SemaphoreType.REGULAR,
+            pltpu.SemaphoreType.REGULAR((ngx,)),
         ],
         compiler_params=pltpu.CompilerParams(
-            collective_id=0, has_side_effects=True, vmem_limit_bytes=67043328
+            collective_id=0, has_side_effects=True, vmem_limit_bytes=60000000
         ),
     )(
         observed, predicted, coherence_mask, block_count, block_owner[:, 0], block_matrix_choice, block_patch,

time: 86.7 us -> 100 us (1.15)
  Pallas kernels: 82.7 us -> 97.9 us
  local copies, waits for them, and re-layouts: 3.02 us -> 1.76 us
    pallas_call x1, Pallas kernels: 82.7 us -> 97.9 us  [per_device(): pl.pallas_call(kernel, out_shape=(out, out), in_specs=[far] * 11, out_spe...]
    unnamed x4 -> x2, local copies, waits for them, and re-layouts: 3.02 us -> 1.76 us
where the time goes in v2:
time: 100 us
  Pallas kernels  97.9 us (98%)
  local copies, waits for them, and re-layouts  1.76 us (2%)
    pallas_call x1, Pallas kernels, per_device(): pl.pallas_call(kernel, out_shape=(out, out), in_specs=[far] * 11, out_spe...  97.9 us

profile of v2, /device:TPU:33, one launch (start us, length us, event | category | flops | bytes accessed | tf_op | source)
XLA Modules:
  0.0 100.3 jit_solution(8232166098393513928)
XLA Ops:
  0.6 97.9 %shard_map.122 = (f32[3,16,32,128]{3,2,1,0:T(8,128)S(1)}, f32[3,16,32,128]{3,2,1,0:T(8,128)S(1)}) custom-call(f32[64,4,256]{2,1,0:T(4,128)} %observed_hbm.1, f32[64,4,256]{2,1,0:T(4,128)} %predicted_hbm.1, s32[64,256]{1,0:T(8,128)} %coherence_hbm.1, s32[64]{0:T(128)} %count_hbm.1, s32[64]{0:T(128)} %bitcast.1, s32[64]{0:T(128)} %table_hbm.1, s32[64]{0:T(128)} %patch_hbm.1, ...), custom_call_target="tpu_custom_call" | custom-call | tf_op jit(solution)/shard_map/pallas_call | solution.py:617
  98.6 0.9 copy.15
  99.4 0.9 copy.16

commit v3 on v2

--- a/solution.py
+++ b/solution.py
@@ -97,7 +97,7 @@
     depths, table,
     fields, w1, w2, div,
     row_out, row_in, ring_in,
-    send_a2a, recv_a2a, send_sem, recv_sem, local_sem, chain, entered,
+    send_a2a, recv_a2a, send_sem, recv_sem, local_sem,
 ):
     pairs = (
         (depth_hbm, depth_ref), (count_hbm, count_ref), (owner_hbm, owner_ref), (table_hbm, table_ref),
@@ -130,21 +130,19 @@
     for z in range(nz):
         own_depths = jnp.where(layer == z, PRE * depth_ref[z], own_depths)
     depths[own_layers, :] = own_depths
-    stiff_x[...] = jnp.zeros(stiff_x.shape, F32)
 
     barrier = pltpu.get_barrier_semaphore()
     peers = [(wrap(gy + k, ngy), gz) for k in range(1, ngy)] + [(wrap(gy + k, ngy), other) for k in range(ngy)]
-    below, above = gx > 0, gx < ngx - 1
+
+    def greet(k, carry):
+        j = wrap(gx - k, ngx)
+        for y in range(ngy):
+            pl.semaphore_signal(barrier, inc=1, device_id=at(j, y, gz))
+        return carry
+
+    lax.fori_loop(1, ngx, greet, 0)
     for y, z in peers:
         pl.semaphore_signal(barrier, inc=1, device_id=at(gx, y, z))
-
-    @pl.when(below)
-    def _():
-        pl.semaphore_signal(barrier, inc=1, device_id=at(gx - 1, gy, gz))
-
-    @pl.when(above)
-    def _():
-        pl.semaphore_signal(barrier, inc=1, device_id=at(gx + 1, gy, gz))
 
     def domain(count):
         r, c = iota((count, lanes), 0), iota((count, lanes), 1)
@@ -162,22 +160,6 @@
     blocks, epochs, pixels = observed_ref.shape
     for fetch in fetches[1:9]:
         fetch.wait()
-
-    pl.semaphore_wait(barrier, len(peers) + below.astype(jnp.int32) + above.astype(jnp.int32))
-
-    @pl.when(below)
-    def _():
-        pl.semaphore_wait(chain, 1)
-
-    @pl.when(above)
-    def _():
-        pl.semaphore_signal(chain, inc=1, device_id=at(gx + 1, gy, gz))
-
-    def announce(j, carry):
-        pl.semaphore_signal(entered.at[gx], inc=1, device_id=at(j, gy, gz))
-        return carry
-
-    lax.fori_loop(0, gx, announce, 0)
 
     for b in range(blocks):
         for k, source in enumerate((count_ref, table_ref, patch_ref, owner_ref)):
@@ -230,6 +212,7 @@
             slots_ref[o, c] = chosen[CAP * o:CAP * (o + 1)]
 
     fetches[10].wait()
+    pl.semaphore_wait(barrier, (ngx - 1) * ngy + len(peers))
 
     def remote(source, target, index, device, arrival=None):
         return pltpu.make_async_remote_copy(
@@ -249,21 +232,17 @@
                     device_id=at(j, y, gz), device_id_type=pl.DeviceIdType.MESH,
                 ).start()
 
-    def post_known(i, carry):
+    def post_pair(i, carry):
         d = ngx // 2 - i
-        down, up = wrap(gx - d, ngx), wrap(gx + d, ngx)
-
-        @pl.when(down < gx)
+        post(wrap(gx - d, ngx), 0)
+
+        @pl.when(d < ngx // 2)
         def _():
-            post(down, 0)
-
-        @pl.when((up < gx) & (d < ngx // 2))
-        def _():
-            post(up, 0)
+            post(wrap(gx + d, ngx), 0)
 
         return carry
 
-    lax.fori_loop(0, ngx // 2, post_known, 0)
+    lax.fori_loop(0, ngx // 2, post_pair, 0)
     post(gx, 1)
 
     x_up, x_down = wrap(gx + 1, ngx), wrap(gx - 1, ngx)
@@ -273,27 +252,13 @@
     to_other = remote(depths.at[own_layers, :], depths.at[own_layers, :], 2, at(gx, gy, other))
     to_other.start()
 
-    @pl.when(below)
-    def _():
-        to_down.start()
-
-    @pl.when(above)
-    def _():
-        to_up.start()
-
+    to_down.start()
+    to_up.start()
     got_slots[me] = slots_ref[me]
     got_choice[me] = choice_ref[me]
 
-    @pl.when(below)
-    def _():
-        to_down.wait_send()
-        to_up.wait_recv()
-
-    @pl.when(above)
-    def _():
-        to_up.wait_send()
-        to_down.wait_recv()
-
+    to_down.wait()
+    to_up.wait()
     to_other.wait()
     low = iota((8, ny), 0) < 4
     for z in range(nz):
@@ -337,13 +302,6 @@
     passed = pl.ds((nz - 4) + 4 * gz, 4)
     layers = remote(coef.at[passed], coef.at[passed], 5, at(gx, gy, other))
     layers.start()
-
-    def post_later(j, carry):
-        pl.semaphore_wait(entered.at[j], 1)
-        post(j, 0)
-        return carry
-
-    lax.fori_loop(gx + 1, ngx, post_later, 0)
 
     for message, buffer in enumerate((slots_ref, choice_ref)):
         part = buffer.at[pl.ds(0, owners - 1)]
@@ -376,7 +334,7 @@
         from_above = roll(roll(tile, bit, 0), -bit * PATCH_Y, 1)
         tile = jnp.where(row_set == chunk_set, tile, jnp.where(row_set, from_above, from_below))
     surf[...] = tile.reshape(3, nx, ny)
-    turned = tile.T
+    turned = jnp.concatenate([tile, jnp.zeros((ny - 3 * nx, ny), F32)], axis=0).T
     border[0] = turned[0:8]
     border[1] = turned[ny - 8:ny]
 
@@ -416,11 +374,11 @@
             [values[0:nx], jnp.where(low_rows, values[nx:nx + 8], values[nx + 8:nx + 16])], axis=0
         )
 
-    blank = jnp.zeros((ny - 16, 3 * nx), F32)
+    blank = jnp.zeros((ny - 16, ny), F32)
 
     def columns_of(place):
         low_side, high_side = halo_y[0, place] + halo_y[1, place], halo_y[0, place + 1] + halo_y[1, place + 1]
-        return jnp.concatenate([low_side, blank, high_side], axis=0).T.reshape(3, nx, ny)
+        return jnp.concatenate([low_side, blank, high_side], axis=0).T[0:3 * nx].reshape(3, nx, ny)
 
     near, upper, lower = columns_of(0), columns_of(2), columns_of(4)
     around = []
@@ -643,9 +601,9 @@
             pltpu.VMEM((owners * CAP, cells), F32),
             pltpu.VMEM((3, nx, ny), F32),
             pltpu.VMEM((3, nx, ny), F32),
-            pltpu.VMEM((2, 8, 3 * nx), F32),
+            pltpu.VMEM((2, 8, ny), F32),
             pltpu.VMEM((2, 2, 3, 8, ny), F32),
-            pltpu.VMEM((2, 6, 8, 3 * nx), F32),
+            pltpu.VMEM((2, 6, 8, ny), F32),
             pltpu.VMEM((2, nz, 8, ny), F32),
             pltpu.VMEM((nz, rows, ny), F32),
             pltpu.VMEM((2, 8, nz * rows), F32),
@@ -665,8 +623,6 @@
             pltpu.SemaphoreType.DMA((copies,)),
             pltpu.SemaphoreType.DMA((copies,)),
             pltpu.SemaphoreType.DMA((11,)),
-            pltpu.SemaphoreType.REGULAR,
-            pltpu.SemaphoreType.REGULAR((ngx,)),
         ],
         compiler_params=pltpu.CompilerParams(
             collective_id=0, has_side_effects=True, vmem_limit_bytes=60000000

time: 100 us -> 84 us (0.84)
  Pallas kernels: 97.9 us -> 81.2 us
    pallas_call x1, Pallas kernels: 97.9 us -> 81.2 us  [per_device(): pl.pallas_call(kernel, out_shape=(out, out), in_specs=[far] * 11, out_spe...]
where the time goes in v3:
time: 84 us; the launch traced here: 83.7 us
  Pallas kernels  81.2 us (97%)
  local copies, waits for them, and re-layouts  1.76 us (2%)
    pallas_call x1, Pallas kernels, per_device(): pl.pallas_call(kernel, out_shape=(out, out), in_specs=[far] * 11, out_spe...  81.2 us
    unnamed x2, local copies, waits for them, and re-layouts  1.76 us

profile of v3, /device:TPU:33, one launch (start us, length us, event | category | flops | bytes accessed | tf_op | source)
XLA Modules:
  0.0 83.7 jit_solution(10402029379055402139)
XLA Ops:
  0.6 81.2 %shard_map.122 = (f32[3,16,32,128]{3,2,1,0:T(8,128)S(1)}, f32[3,16,32,128]{3,2,1,0:T(8,128)S(1)}) custom-call(f32[64,4,256]{2,1,0:T(4,128)} %observed_hbm.1, f32[64,4,256]{2,1,0:T(4,128)} %predicted_hbm.1, s32[64,256]{1,0:T(8,128)} %coherence_hbm.1, s32[64]{0:T(128)} %count_hbm.1, s32[64]{0:T(128)} %bitcast.1, s32[64]{0:T(128)} %table_hbm.1, s32[64]{0:T(128)} %patch_hbm.1, ...), custom_call_target="tpu_custom_call" | custom-call | tf_op jit(solution)/shard_map/pallas_call | solution.py:575
  81.9 0.9 %copy.15 = f32[3,16,32,128]{3,2,1,0:T(8,128)} copy(f32[3,16,32,128]{3,2,1,0:T(8,128)S(1)} %get-tuple-element.2) | data formatting | bytes 1572864
  82.8 0.9 %copy.16 = f32[3,16,32,128]{3,2,1,0:T(8,128)} copy(f32[3,16,32,128]{3,2,1,0:T(8,128)S(1)} %get-tuple-element.3) | data formatting | bytes 1572864

commit v4 on v3

--- a/solution.py
+++ b/solution.py
@@ -33,6 +33,17 @@
 
 def iota(shape, axis):
     return lax.broadcasted_iota(jnp.int32, shape, axis)
+
+
+def pairwise(start, stop, body):
+    def trip(k, carry):
+        body(start + 2 * k, None)
+        body(start + 2 * k + 1, None)
+        return carry
+
+    lax.fori_loop(0, (stop - start) // 2, trip, 0)
+    if (stop - start) % 2:
+        body(stop - 1, None)
 
 
 def product(first, second, moments):
@@ -173,13 +184,15 @@
     res = resid[...]
     row_block, row_place = iota((blocks, epochs * blocks), 0), iota((blocks, epochs * blocks), 1)
     own_rows = row_place // epochs == row_block
+    mixes = []
     for c in range(3):
         mix = jnp.zeros((blocks, epochs * blocks), F32)
         for e in range(epochs):
             mix = jnp.where(own_rows & (row_place % epochs == e), look_ref[e, c], mix)
-        coeffs[c * blocks:(c + 1) * blocks, :] = jnp.dot(
-            mix, res, precision=HIGHEST, preferred_element_type=F32
-        )
+        mixes.append(mix)
+    coeffs[...] = jnp.dot(
+        jnp.concatenate(mixes, axis=0), res, precision=HIGHEST, preferred_element_type=F32
+    )
     mass = jnp.sum(jnp.sum(res * res, axis=0, keepdims=True), axis=1, keepdims=True)
     weight = jnp.sum(jnp.sum(valid[...], axis=0, keepdims=True), axis=1, keepdims=True)
 
@@ -203,13 +216,13 @@
     for t in range(weights.shape[0]):
         taken = jnp.where(which == t, rounded, 0.0).astype(jnp.bfloat16)
         total_sums = total_sums + jnp.dot(taken, weights[t], preferred_element_type=F32)
+    chosen = lax.dot_general(
+        select, jnp.concatenate([total_sums[c * blocks:(c + 1) * blocks] for c in range(3)], axis=1),
+        (((0,), (0,)), ((), ())), precision=HIGHEST, preferred_element_type=F32,
+    )
     for c in range(3):
-        chosen = lax.dot_general(
-            select, total_sums[c * blocks:(c + 1) * blocks], (((0,), (0,)), ((), ())),
-            precision=HIGHEST, preferred_element_type=F32,
-        )
         for o in range(owners):
-            slots_ref[o, c] = chosen[CAP * o:CAP * (o + 1)]
+            slots_ref[o, c] = chosen[CAP * o:CAP * (o + 1), c * ny:(c + 1) * ny]
 
     fetches[10].wait()
     pl.semaphore_wait(barrier, (ngx - 1) * ngy + len(peers))
@@ -221,6 +234,15 @@
             device_id=device, device_id_type=pl.DeviceIdType.MESH,
         )
 
+    x_up, x_down = wrap(gx + 1, ngx), wrap(gx - 1, ngx)
+    y_up, y_down = wrap(gy + 1, ngy), wrap(gy - 1, ngy)
+    to_down = remote(stiff_ref.at[:, pl.ds(0, 8), :], stiff_x.at[0], 0, at(x_down, gy, gz))
+    to_up = remote(stiff_ref.at[:, pl.ds(nx - 8, 8), :], stiff_x.at[1], 1, at(x_up, gy, gz))
+    to_other = remote(depths.at[own_layers, :], depths.at[own_layers, :], 2, at(gx, gy, other))
+    to_other.start()
+
+    to_down.start()
+    to_up.start()
     def post(j, first):
         for k in range(first, ngy):
             y = wrap(gy + k, ngy)
@@ -245,21 +267,13 @@
     lax.fori_loop(0, ngx // 2, post_pair, 0)
     post(gx, 1)
 
-    x_up, x_down = wrap(gx + 1, ngx), wrap(gx - 1, ngx)
-    y_up, y_down = wrap(gy + 1, ngy), wrap(gy - 1, ngy)
-    to_down = remote(stiff_ref.at[:, pl.ds(0, 8), :], stiff_x.at[0], 0, at(x_down, gy, gz))
-    to_up = remote(stiff_ref.at[:, pl.ds(nx - 8, 8), :], stiff_x.at[1], 1, at(x_up, gy, gz))
-    to_other = remote(depths.at[own_layers, :], depths.at[own_layers, :], 2, at(gx, gy, other))
-    to_other.start()
-
-    to_down.start()
-    to_up.start()
     got_slots[me] = slots_ref[me]
     got_choice[me] = choice_ref[me]
 
-    to_down.wait()
-    to_up.wait()
-    to_other.wait()
+    to_down.wait_recv()
+    to_up.wait_recv()
+    to_other.wait_recv()
+    sent = [to_down, to_up, to_other]
     low = iota((8, ny), 0) < 4
     for z in range(nz):
         wide_stiff[z, 0:nx, :] = stiff_ref[z]
@@ -292,7 +306,8 @@
             table[k, z] = values[z + 8:z + 9]
 
     for copy in strips:
-        copy.wait()
+        copy.wait_recv()
+    sent = sent + strips
     filler = jnp.zeros((ny - 16, nz * rows), F32)
     beside = jnp.concatenate([strip_in[0], filler, strip_in[1]], axis=0).T.reshape(nz, rows, ny)
     base = nz * gz
@@ -303,27 +318,24 @@
     layers = remote(coef.at[passed], coef.at[passed], 5, at(gx, gy, other))
     layers.start()
 
-    for message, buffer in enumerate((slots_ref, choice_ref)):
-        part = buffer.at[pl.ds(0, owners - 1)]
-        pltpu.make_async_copy(part, part, send_a2a.at[message]).wait()
     for message, buffer in enumerate((got_slots, got_choice)):
         part = buffer.at[pl.ds(0, owners - 1)]
         pltpu.make_async_copy(part, part, recv_a2a.at[message]).wait()
     own_slot = iota((CAP, ny), 1) // (ny // CAP) == iota((CAP, ny), 0)
     for o in range(owners):
         for c in range(3):
-            flat_slots[c, CAP * o:CAP * (o + 1), :] = got_slots[o, c]
+            flat_slots[CAP * o:CAP * (o + 1), c * ny:(c + 1) * ny] = got_slots[o, c]
         flat_choice[CAP * o:CAP * (o + 1), :] = jnp.where(own_slot, got_choice[o], 0.0)
     picked = flat_choice[...]
+    spread = lax.dot_general(
+        picked, flat_slots[...], (((0,), (0,)), ((), ())), precision=HIGHEST, preferred_element_type=F32
+    )
+    depth_places = ny // CAP
     tiles = []
     for c in range(3):
-        spread = lax.dot_general(
-            picked, flat_slots[c], (((0,), (0,)), ((), ())), precision=HIGHEST, preferred_element_type=F32
-        )
-        depth_places = ny // CAP
-        placed = spread[0:depth_places]
+        placed = spread[0:depth_places, c * ny:(c + 1) * ny]
         for j in range(1, CAP):
-            placed = placed + spread[j * depth_places:(j + 1) * depth_places]
+            placed = placed + spread[j * depth_places:(j + 1) * depth_places, c * ny:(c + 1) * ny]
         tiles.append(placed)
     tile = jnp.concatenate(tiles, axis=0)
     sub = lax.rem(iota(tile.shape, 0), 8)
@@ -359,12 +371,11 @@
             copy = remote(source, target.at[gz, place], 7 + i * count + k, at(x, y, z), 7 + gz * count + k)
             copy.start()
             started.append(copy)
-    swap.wait()
+    swap.wait_recv()
     for k, (source, target, place, x, y) in enumerate(ways):
         for i in range(2):
             remote(source, target.at[i, place], 7 + i * count + k, at(x, y, gz)).wait_recv()
-    for copy in started:
-        copy.wait_send()
+    sent = sent + [swap] + started
     mask_tall = domain(tall)
     mask = domain(rows)
     low_rows = iota((8, lanes), 0) < 4
@@ -403,7 +414,8 @@
             fields[3 + c] = mask * packed(0.125 * beside_xy)
     fields[8] = packed(flux)
 
-    layers.wait()
+    layers.wait_recv()
+    sent = sent + [layers]
 
     def first_layer(i, carry):
         z = (nz - 4) * gz + i
@@ -414,7 +426,7 @@
         w1[2, z + 1] = mask * (fields[2] * (own - value[4])) - value[0] * fields[5] - value[3] * fields[8]
         return carry
 
-    lax.fori_loop(0, nz + 4, first_layer, 0)
+    pairwise(0, nz + 4, first_layer)
 
     def spread_of(source, start, amount):
         def layer(i, carry):
@@ -426,7 +438,7 @@
             )
             return carry
 
-        lax.fori_loop(0, amount, layer, 0)
+        pairwise(0, amount, layer)
 
     spread_of(w1, (nz - 3) * gz, nz + 3)
 
@@ -442,7 +454,7 @@
             w2[c, z + 1] = mask * (own * v - 0.125 * total - (1.0 / 64.0) * slope)
         return carry
 
-    lax.fori_loop(0, nz + 2, second_layer, 0)
+    pairwise(0, nz + 2, second_layer)
 
     spread_of(w2, (nz - 1) * gz, nz + 1)
 
@@ -507,9 +519,10 @@
         copy = remote(row_out.at[0], row_in.at[slot], base + k, at(gx, y, z))
         copy.start()
         started.append(copy)
-    lax.fori_loop(0, early_layers, third_layer, 0)
+    pairwise(0, early_layers, third_layer)
     for copy in started:
-        copy.wait()
+        copy.wait_recv()
+    sent = sent + started
     message = row_in[0]
     for k in range(1, 2 * ngy):
         message = message + row_in[k]
@@ -521,9 +534,10 @@
         copy = remote(row_out.at[1], ring_in.at[gx], first_index + k - 1, at(wrap(gx + k, ngx), gy, gz))
         copy.start()
         started.append(copy)
-    lax.fori_loop(early_layers, nz, third_layer, 0)
+    pairwise(early_layers, nz, third_layer)
     for copy in started:
-        copy.wait()
+        copy.wait_recv()
+    sent = sent + started
     message = ring_in[0]
     for k in range(1, ngx):
         message = message + ring_in[k]
@@ -545,7 +559,12 @@
             res_ref[c, i] = residual[0] * zeroth + residual[1] * one + residual[2] * two + residual[3] * third
         return carry
 
-    lax.fori_loop(0, nz, finish, 0)
+    pairwise(0, nz, finish)
+    for copy in sent:
+        copy.wait_send()
+    for message, buffer in enumerate((slots_ref, choice_ref)):
+        part = buffer.at[pl.ds(0, owners - 1)]
+        pltpu.make_async_copy(part, part, send_a2a.at[message]).wait()
 
 
 def per_device(
@@ -597,7 +616,7 @@
             pltpu.VMEM((owners, 1, cells), F32),
             pltpu.VMEM((owners, 3, CAP, cells), F32),
             pltpu.VMEM((owners, 1, cells), F32),
-            pltpu.VMEM((3, owners * CAP, cells), F32),
+            pltpu.VMEM((owners * CAP, 3 * cells), F32),
             pltpu.VMEM((owners * CAP, cells), F32),
             pltpu.VMEM((3, nx, ny), F32),
             pltpu.VMEM((3, nx, ny), F32),

time: 84 us -> 79.7 us (0.949)
  Pallas kernels: 81.2 us -> 76.9 us
    pallas_call x1, Pallas kernels: 81.2 us -> 76.9 us  [per_device(): pl.pallas_call(kernel, out_shape=(out, out), in_specs=[far] * 11, out_spe...]
where the time goes in v4:
time: 79.7 us; the launch traced here: 79.3 us
  Pallas kernels  76.9 us (96%)
  local copies, waits for them, and re-layouts  1.76 us (2%)
    pallas_call x1, Pallas kernels, per_device(): pl.pallas_call(kernel, out_shape=(out, out), in_specs=[far] * 11, out_spe...  76.9 us
    unnamed x2, local copies, waits for them, and re-layouts  1.76 us

profile of v4, /device:TPU:33, one launch (start us, length us, event | category | flops | bytes accessed | tf_op | source)
XLA Modules:
  0.0 79.3 jit_solution(148549525706067441)
XLA Ops:
  0.6 76.9 %shard_map.122 = (f32[3,16,32,128]{3,2,1,0:T(8,128)S(1)}, f32[3,16,32,128]{3,2,1,0:T(8,128)S(1)}) custom-call(f32[64,4,256]{2,1,0:T(4,128)} %observed_hbm.1, f32[64,4,256]{2,1,0:T(4,128)} %predicted_hbm.1, s32[64,256]{1,0:T(8,128)} %coherence_hbm.1, s32[64]{0:T(128)} %count_hbm.1, s32[64]{0:T(128)} %bitcast.1, s32[64]{0:T(128)} %table_hbm.1, s32[64]{0:T(128)} %patch_hbm.1, ...), custom_call_target="tpu_custom_call" | custom-call | tf_op jit(solution)/shard_map/pallas_call | solution.py:594
  77.6 0.9 %copy.15 = f32[3,16,32,128]{3,2,1,0:T(8,128)} copy(f32[3,16,32,128]{3,2,1,0:T(8,128)S(1)} %get-tuple-element.2) | data formatting | bytes 1572864
  78.5 0.9 %copy.16 = f32[3,16,32,128]{3,2,1,0:T(8,128)} copy(f32[3,16,32,128]{3,2,1,0:T(8,128)S(1)} %get-tuple-element.3) | data formatting | bytes 1572864

commit v5 on v4

--- a/solution.py
+++ b/solution.py
@@ -104,7 +104,7 @@
     numbers, valid, resid, coeffs, slots_ref, choice_ref,
     got_slots, got_choice, flat_slots, flat_choice,
     surf, surf_other, border, halo_x, halo_y,
-    stiff_x, wide_stiff, strip_out, strip_in, coef,
+    stiff_edge, stiff_x, wide_stiff, strip_out, strip_in, coef,
     depths, table,
     fields, w1, w2, div,
     row_out, row_in, ring_in,
@@ -134,6 +134,20 @@
         return lax.rem(value + count, count)
 
     depths[...] = jnp.zeros(depths.shape, F32)
+
+    barrier = pltpu.get_barrier_semaphore()
+    peers = [(wrap(gy + k, ngy), gz) for k in range(1, ngy)] + [(wrap(gy + k, ngy), other) for k in range(ngy)]
+
+    def greet(k, carry):
+        j = wrap(gx - k, ngx)
+        for y in range(ngy):
+            pl.semaphore_signal(barrier, inc=1, device_id=at(j, y, gz))
+        return carry
+
+    lax.fori_loop(1, ngx, greet, 0)
+    for y, z in peers:
+        pl.semaphore_signal(barrier, inc=1, device_id=at(gx, y, z))
+
     own_layers = pl.ds(pl.multiple_of(8 + nz * gz, 8), nz)
     fetches[0].wait()
     layer = iota((nz, lanes), 0)
@@ -141,19 +155,6 @@
     for z in range(nz):
         own_depths = jnp.where(layer == z, PRE * depth_ref[z], own_depths)
     depths[own_layers, :] = own_depths
-
-    barrier = pltpu.get_barrier_semaphore()
-    peers = [(wrap(gy + k, ngy), gz) for k in range(1, ngy)] + [(wrap(gy + k, ngy), other) for k in range(ngy)]
-
-    def greet(k, carry):
-        j = wrap(gx - k, ngx)
-        for y in range(ngy):
-            pl.semaphore_signal(barrier, inc=1, device_id=at(j, y, gz))
-        return carry
-
-    lax.fori_loop(1, ngx, greet, 0)
-    for y, z in peers:
-        pl.semaphore_signal(barrier, inc=1, device_id=at(gx, y, z))
 
     def domain(count):
         r, c = iota((count, lanes), 0), iota((count, lanes), 1)
@@ -212,6 +213,10 @@
     which = jnp.concatenate([numbers[1]] * 3, axis=0)
     which = jnp.concatenate([which] * (pixels // ny), axis=1)
     fetches[9].wait()
+    fetches[10].wait()
+    for z in range(nz):
+        stiff_edge[0, z] = stiff_ref[z, 0:4]
+        stiff_edge[1, z] = stiff_ref[z, nx - 4:nx]
     total_sums = jnp.zeros((3 * blocks, ny), F32)
     for t in range(weights.shape[0]):
         taken = jnp.where(which == t, rounded, 0.0).astype(jnp.bfloat16)
@@ -224,7 +229,6 @@
         for o in range(owners):
             slots_ref[o, c] = chosen[CAP * o:CAP * (o + 1), c * ny:(c + 1) * ny]
 
-    fetches[10].wait()
     pl.semaphore_wait(barrier, (ngx - 1) * ngy + len(peers))
 
     def remote(source, target, index, device, arrival=None):
@@ -236,8 +240,8 @@
 
     x_up, x_down = wrap(gx + 1, ngx), wrap(gx - 1, ngx)
     y_up, y_down = wrap(gy + 1, ngy), wrap(gy - 1, ngy)
-    to_down = remote(stiff_ref.at[:, pl.ds(0, 8), :], stiff_x.at[0], 0, at(x_down, gy, gz))
-    to_up = remote(stiff_ref.at[:, pl.ds(nx - 8, 8), :], stiff_x.at[1], 1, at(x_up, gy, gz))
+    to_down = remote(stiff_edge.at[0], stiff_x.at[0], 0, at(x_down, gy, gz))
+    to_up = remote(stiff_edge.at[1], stiff_x.at[1], 1, at(x_up, gy, gz))
     to_other = remote(depths.at[own_layers, :], depths.at[own_layers, :], 2, at(gx, gy, other))
     to_other.start()
 
@@ -274,10 +278,10 @@
     to_up.wait_recv()
     to_other.wait_recv()
     sent = [to_down, to_up, to_other]
-    low = iota((8, ny), 0) < 4
     for z in range(nz):
         wide_stiff[z, 0:nx, :] = stiff_ref[z]
-        wide_stiff[z, nx:rows, :] = jnp.where(low, stiff_x[0, z], stiff_x[1, z])
+        wide_stiff[z, nx:nx + 4, :] = stiff_x[0, z]
+        wide_stiff[z, nx + 4:rows, :] = stiff_x[1, z]
     turned = wide_stiff[...].reshape(nz * rows, ny).T
     strip_out[0] = turned[0:8]
     strip_out[1] = turned[ny - 8:ny]
@@ -623,7 +627,8 @@
             pltpu.VMEM((2, 8, ny), F32),
             pltpu.VMEM((2, 2, 3, 8, ny), F32),
             pltpu.VMEM((2, 6, 8, ny), F32),
-            pltpu.VMEM((2, nz, 8, ny), F32),
+            pltpu.VMEM((2, nz, 4, ny), F32),
+            pltpu.VMEM((2, nz, 4, ny), F32),
             pltpu.VMEM((nz, rows, ny), F32),
             pltpu.VMEM((2, 8, nz * rows), F32),
             pltpu.VMEM((2, 8, nz * rows), F32),

time: 79.7 us -> 78.2 us (0.981)
  Pallas kernels: 76.9 us -> 75.5 us
    pallas_call x1, Pallas kernels: 76.9 us -> 75.5 us  [per_device(): pl.pallas_call(kernel, out_shape=(out, out), in_specs=[far] * 11, out_spe...]
where the time goes in v5:
time: 78.2 us; the launch traced here: 77.9 us
  Pallas kernels  75.5 us (97%)
  local copies, waits for them, and re-layouts  1.76 us (2%)
    pallas_call x1, Pallas kernels, per_device(): pl.pallas_call(kernel, out_shape=(out, out), in_specs=[far] * 11, out_spe...  75.5 us
    unnamed x2, local copies, waits for them, and re-layouts  1.76 us

profile of v5, /device:TPU:33, one launch (start us, length us, event | category | flops | bytes accessed | tf_op | source)
XLA Modules:
  0.0 77.9 jit_solution(12963740082202318493)
XLA Ops:
  0.6 75.5 %shard_map.122 = (f32[3,16,32,128]{3,2,1,0:T(8,128)S(1)}, f32[3,16,32,128]{3,2,1,0:T(8,128)S(1)}) custom-call(f32[64,4,256]{2,1,0:T(4,128)} %observed_hbm.1, f32[64,4,256]{2,1,0:T(4,128)} %predicted_hbm.1, s32[64,256]{1,0:T(8,128)} %coherence_hbm.1, s32[64]{0:T(128)} %count_hbm.1, s32[64]{0:T(128)} %bitcast.1, s32[64]{0:T(128)} %table_hbm.1, s32[64]{0:T(128)} %patch_hbm.1, ...), custom_call_target="tpu_custom_call" | custom-call | tf_op jit(solution)/shard_map/pallas_call | solution.py:598
  76.1 0.9 %copy.15 = f32[3,16,32,128]{3,2,1,0:T(8,128)} copy(f32[3,16,32,128]{3,2,1,0:T(8,128)S(1)} %get-tuple-element.2) | data formatting | bytes 1572864
  77.0 0.9 %copy.16 = f32[3,16,32,128]{3,2,1,0:T(8,128)} copy(f32[3,16,32,128]{3,2,1,0:T(8,128)S(1)} %get-tuple-element.3) | data formatting | bytes 1572864

commit v6 on v5

--- a/solution.py
+++ b/solution.py
@@ -460,8 +460,6 @@
 
     pairwise(0, nz + 2, second_layer)
 
-    spread_of(w2, (nz - 1) * gz, nz + 1)
-
     def folded(values):
         total = values[0:8]
         for k in range(8, nx, 8):
@@ -472,22 +470,30 @@
         z = nz * gz + i
         own = coef[z, 0:nx, 0:ny]
         d_now = table[0, z, :, 0:ny]
-        here = div[z + 1, 0:nx, 0:ny]
         terms = [None] * MOMENTS
-        terms[MOMENTS - 1] = (1.0 / 64.0) * (here * here)
+        here = w2[2, z + 2, 0:nx, 0:ny] - w2[2, z, 0:nx, 0:ny]
         for c in range(3):
             v = w2[c, z + 1, 0:nx, 0:ny]
-            total = ahead(w2[c, z + 1, :, 0:ny], 0)[0:nx] + ahead(w2[c, z + 1, 0:nx, :], 1)[:, 0:ny]
-            total = total + w2[c, z + 2, 0:nx, 0:ny]
+            vx, vy = w2[c, z + 1, :, 0:ny], w2[c, z + 1, 0:nx, :]
+            next_x, next_y = ahead(vx, 0)[0:nx], ahead(vy, 1)[:, 0:ny]
+            total = (next_x + next_y) + w2[c, z + 2, 0:nx, 0:ny]
+            if c == 0:
+                here = here + (next_x - behind(vx, 0)[0:nx])
+            elif c == 1:
+                here = here + (next_y - behind(vy, 1)[:, 0:ny])
             zeroth = d_now * fields[c, 0:nx, 0:ny]
             one = w1[c, z + 1, 0:nx, 0:ny]
             for k, term in enumerate(
                 (zeroth * zeroth, zeroth * one, one * one, one * v, v * v, v * (own * v - 0.25 * total))
             ):
                 terms[k] = term if terms[k] is None else terms[k] + term
+        terms[MOMENTS - 1] = terms[MOMENTS - 1] + (1.0 / 64.0) * (here * here)
         return tuple(s + folded(t) for s, t in zip(sums, terms))
 
-    sums = lax.fori_loop(0, nz, gather_moments, tuple(jnp.zeros((8, ny), F32) for _ in range(MOMENTS)))
+    sums = lax.fori_loop(
+        0, nz // 2, lambda k, sums: gather_moments(2 * k + 1, gather_moments(2 * k, sums)),
+        tuple(jnp.zeros((8, ny), F32) for _ in range(MOMENTS)),
+    )
 
     def third_layer(i, carry):
         z = nz * gz + i
@@ -507,7 +513,7 @@
             res_ref[c, i] = own * v - 0.125 * total - (1.0 / 64.0) * slope
         return carry
 
-    early_layers = (3 * nz) // 8
+    early_layers = nz // 4
 
     lane = iota((1, ny), 1)
     message = jnp.where(lane == MOMENTS, mass, 0.0) + jnp.where(lane == MOMENTS + 1, weight, 0.0)
@@ -523,6 +529,7 @@
         copy = remote(row_out.at[0], row_in.at[slot], base + k, at(gx, y, z))
         copy.start()
         started.append(copy)
+    spread_of(w2, (nz - 1) * gz, nz + 1)
     pairwise(0, early_layers, third_layer)
     for copy in started:
         copy.wait_recv()

time: 78.2 us -> 76.6 us (0.980)
  Pallas kernels: 75.5 us -> 73.9 us
    pallas_call x1, Pallas kernels: 75.5 us -> 73.9 us  [per_device(): pl.pallas_call(kernel, out_shape=(out, out), in_specs=[far] * 11, out_spe...]
where the time goes in v6:
time: 76.6 us; the launch traced here: 76.3 us
  Pallas kernels  73.9 us (96%)
  local copies, waits for them, and re-layouts  1.76 us (2%)
    pallas_call x1, Pallas kernels, per_device(): pl.pallas_call(kernel, out_shape=(out, out), in_specs=[far] * 11, out_spe...  73.9 us
    unnamed x2, local copies, waits for them, and re-layouts  1.76 us

profile of v6, /device:TPU:33, one launch (start us, length us, event | category | flops | bytes accessed | tf_op | source)
XLA Modules:
  0.0 76.3 jit_solution(1581533163559272012)
XLA Ops:
  0.6 73.9 %shard_map.122 = (f32[3,16,32,128]{3,2,1,0:T(8,128)S(1)}, f32[3,16,32,128]{3,2,1,0:T(8,128)S(1)}) custom-call(f32[64,4,256]{2,1,0:T(4,128)} %observed_hbm.1, f32[64,4,256]{2,1,0:T(4,128)} %predicted_hbm.1, s32[64,256]{1,0:T(8,128)} %coherence_hbm.1, s32[64]{0:T(128)} %count_hbm.1, s32[64]{0:T(128)} %bitcast.1, s32[64]{0:T(128)} %table_hbm.1, s32[64]{0:T(128)} %patch_hbm.1, ...), custom_call_target="tpu_custom_call" | custom-call | tf_op jit(solution)/shard_map/pallas_call | solution.py:605
  74.5 0.9 %copy.15 = f32[3,16,32,128]{3,2,1,0:T(8,128)} copy(f32[3,16,32,128]{3,2,1,0:T(8,128)S(1)} %get-tuple-element.2) | data formatting | bytes 1572864
  75.4 0.9 %copy.16 = f32[3,16,32,128]{3,2,1,0:T(8,128)} copy(f32[3,16,32,128]{3,2,1,0:T(8,128)S(1)} %get-tuple-element.3) | data formatting | bytes 1572864

commit v7 on v6

--- a/solution.py
+++ b/solution.py
@@ -136,7 +136,8 @@
     depths[...] = jnp.zeros(depths.shape, F32)
 
     barrier = pltpu.get_barrier_semaphore()
-    peers = [(wrap(gy + k, ngy), gz) for k in range(1, ngy)] + [(wrap(gy + k, ngy), other) for k in range(ngy)]
+    far_first = sorted(range(ngy), key=lambda k: -min(k, ngy - k))
+    peers = [(wrap(gy + k, ngy), z) for k in far_first for z in (gz, other) if k or z is other]
 
     def greet(k, carry):
         j = wrap(gx - k, ngx)
@@ -541,7 +542,7 @@
     ring_in[gx] = message
     first_index = base + len(peers)
     started = []
-    for k in range(1, ngx):
+    for k in sorted(range(1, ngx), key=lambda k: -min(k, ngx - k)):
         copy = remote(row_out.at[1], ring_in.at[gx], first_index + k - 1, at(wrap(gx + k, ngx), gy, gz))
         copy.start()
         started.append(copy)

time: 76.6 us -> 76.5 us (level)
  no operation moved by 1% of the time
where the time goes in v7:
time: 76.5 us; the launch traced here: 76.3 us
  Pallas kernels  73.9 us (97%)
  local copies, waits for them, and re-layouts  1.76 us (2%)
    pallas_call x1, Pallas kernels, per_device(): pl.pallas_call(kernel, out_shape=(out, out), in_specs=[far] * 11, out_spe...  73.9 us
    unnamed x2, local copies, waits for them, and re-layouts  1.76 us

profile of v7, /device:TPU:33, one launch (start us, length us, event | category | flops | bytes accessed | tf_op | source)
XLA Modules:
  0.0 76.3 jit_solution(6939255300362373071)
XLA Ops:
  0.6 73.9 %shard_map.122 = (f32[3,16,32,128]{3,2,1,0:T(8,128)S(1)}, f32[3,16,32,128]{3,2,1,0:T(8,128)S(1)}) custom-call(f32[64,4,256]{2,1,0:T(4,128)} %observed_hbm.1, f32[64,4,256]{2,1,0:T(4,128)} %predicted_hbm.1, s32[64,256]{1,0:T(8,128)} %coherence_hbm.1, s32[64]{0:T(128)} %count_hbm.1, s32[64]{0:T(128)} %bitcast.1, s32[64]{0:T(128)} %table_hbm.1, s32[64]{0:T(128)} %patch_hbm.1, ...), custom_call_target="tpu_custom_call" | custom-call | tf_op jit(solution)/shard_map/pallas_call | solution.py:606
  74.5 0.9 %copy.15 = f32[3,16,32,128]{3,2,1,0:T(8,128)} copy(f32[3,16,32,128]{3,2,1,0:T(8,128)S(1)} %get-tuple-element.2) | data formatting | bytes 1572864
  75.4 0.9 %copy.16 = f32[3,16,32,128]{3,2,1,0:T(8,128)} copy(f32[3,16,32,128]{3,2,1,0:T(8,128)S(1)} %get-tuple-element.3) | data formatting | bytes 1572864
